TPU v7x, 512 devices: a whole 4x4x16 slice. The times are simulated.
512 devices in a mesh: row: 32 (over z_lo, x), col: 16 (over z_hi, y, core).
Axes of the slice: x: 4, y: 4, z: 16 (z_hi: 2, z_lo: 8; z = z_hi * 8 + z_lo), core: 2. Of those that a mesh axis runs over, the one named last changes fastest.
Arguments:
- noisy: float32 [1024, 32768], P('row', 'col'), may hold values from -9 to 9
Outputs:
- denoised: float32 [1024, 32768], P('row', 'col')
- gap: float32 [4], replicated
All inputs are finite; a program needn't handle non-finite values.
Results may differ from a plain program's by a relative error of at most 0.0003.
Values sent between devices are 32-bit elements; how exact they have to be, the bound alone decides.
A program may use at most 64 MiB of HBM per device.

v0:
```python
import jax
import jax.numpy as jnp
from jax import lax
from jax.sharding import Mesh
from jax.sharding import PartitionSpec as P

ITERS = 4
ROW = ("row_0", "row_1")
COL = ("col_0", "col_1", "col_2")
ROW_COL = ("row_0", "row_1", "col_0", "col_1", "col_2")


fidelity = 8.0
primal_step = 0.35
dual_step = 0.35


def with_halo(shard, sides, width):
    for axis, dim in sides:
        size, length = (lax.axis_size(axis), shard.shape[dim])
        up = [(i, (i + 1) % size) for i in range(size - 1)]
        down = [(j, i) for i, j in up]
        last = lax.slice_in_dim(shard, length - width, length, axis=dim)
        first = lax.slice_in_dim(shard, 0, width, axis=dim)
        before = lax.ppermute(last, axis, up)
        after = lax.ppermute(first, axis, down)
        shard = jnp.concatenate([before, shard, after], axis=dim)
    return shard


def by_axis(shard, axes):
    for axis in axes:
        shard = lax.psum(shard, axis)
    return shard


def gap_piece(edge_rows, edge_cols, primal, noisy, diverged):
    return jnp.sum(jnp.sqrt(edge_rows * edge_rows + edge_cols * edge_cols)) + jnp.sum(
        0.5 * fidelity * (primal - noisy) ** 2
        + noisy * diverged
        + diverged * diverged / (2.0 * fidelity)
    )


def deep_run(noisy):
    tile_rows, tile_cols = noisy.shape
    rows_all = lax.axis_size(ROW) * tile_rows
    cols_all = lax.axis_size(COL) * tile_cols
    margin = ITERS + 1
    framed = with_halo(noisy, ((ROW, 0), (COL, 1)), margin)
    global_rows = (
        lax.axis_index(ROW) * tile_rows
        - margin
        + jnp.arange(tile_rows + 2 * margin, dtype=jnp.int32)
    )
    global_cols = (
        lax.axis_index(COL) * tile_cols
        - margin
        + jnp.arange(tile_cols + 2 * margin, dtype=jnp.int32)
    )
    rows_inside = (global_rows >= 0) & (global_rows < rows_all)
    rows_inner = (global_rows >= 0) & (global_rows < rows_all - 1)
    cols_inside = (global_cols >= 0) & (global_cols < cols_all)
    cols_inner = (global_cols >= 0) & (global_cols < cols_all - 1)
    mask_rows = (rows_inner[:, None] & cols_inside[None, :]).astype(jnp.float32)
    mask_cols = (rows_inside[:, None] & cols_inner[None, :]).astype(jnp.float32)
    frame_rows, frame_cols = framed.shape

    def masked_grads(field):
        row_diff = jnp.concatenate(
            [field[1:] - field[:-1], jnp.zeros((1, frame_cols), jnp.float32)], 0
        )
        col_diff = jnp.concatenate(
            [field[:, 1:] - field[:, :-1], jnp.zeros((frame_rows, 1), jnp.float32)], 1
        )
        return (row_diff * mask_rows, col_diff * mask_cols)

    primal = framed
    previous = framed
    dual = jnp.zeros((2,) + framed.shape, jnp.float32)
    pieces = []
    for iteration in range(ITERS):
        extrapolated = 2.0 * primal - previous
        grad_rows, grad_cols = masked_grads(extrapolated)
        trial = dual + dual_step * jnp.stack([grad_rows, grad_cols])
        shrink = 1.0 / jnp.maximum(1.0, jnp.sqrt(trial[0] * trial[0] + trial[1] * trial[1]))
        dual = trial * shrink
        diverged = (
            dual[0]
            - jnp.concatenate([jnp.zeros((1, frame_cols), jnp.float32), dual[0, :-1]], 0)
            + dual[1]
            - jnp.concatenate([jnp.zeros((frame_rows, 1), jnp.float32), dual[1, :, :-1]], 1)
        )
        updated = (primal + primal_step * diverged + primal_step * fidelity * framed) / (
            1.0 + primal_step * fidelity
        )
        previous = primal
        primal = updated
        edge_rows, edge_cols = masked_grads(primal)
        owned_r = slice(margin, margin + tile_rows)
        owned_c = slice(margin, margin + tile_cols)
        pieces.append(
            gap_piece(
                edge_rows[owned_r, owned_c],
                edge_cols[owned_r, owned_c],
                primal[owned_r, owned_c],
                noisy,
                diverged[owned_r, owned_c],
            )
        )
    return (primal[margin : margin + tile_rows, margin : margin + tile_cols], pieces)


def on_device(noisy):
    cells = lax.axis_size(ROW) * noisy.shape[0] * lax.axis_size(COL) * noisy.shape[1]
    primal, pieces = deep_run(noisy)
    gap = by_axis(jnp.stack(pieces), ROW_COL) / cells
    return (primal, gap)


def solution(mesh):
    torus = Mesh(mesh.devices.reshape(8, 4, 2, 4, 2), ("row_0", "row_1", "col_0", "col_1", "col_2"))
    return jax.shard_map(
        on_device,
        mesh=torus,
        in_specs=(P(ROW, COL),),
        out_specs=(P(ROW, COL), P()),
        check_vma=False,
    )
```

profile of v0, /device:TPU:1, one launch (start us, length us, event | category | flops | bytes accessed | tf_op | source)
XLA Modules:
  0.0 118.6 jit_solution(13011369884884892752)
XLA Ops:
  0.6 0.9 fusion.92
  1.6 1.3 %collective-permute-start.1 = (f32[5,2048]{1,0:T(8,128)S(1)}, f32[5,2048]{1,0:T(8,128)S(1)}, u32[]{:S(2)}, u32[]{:S(2)}) collective-permute-start(f32[5,2048]{1,0:T(8,128)S(1)} %get-tuple-element.24), channel_id=1, source_target_pairs={{16,0},{32,16},{48,32},{64,48},{80,64},{96,80},{112,96},{128,112},... | collective-permute-start | bytes 122888 | tf_op jit(solution)/shard_map/ppermute | solution.py:26
  2.9 4.6 %collective-permute-start = (f32[5,2048]{1,0:T(8,128)S(1)}, f32[5,2048]{1,0:T(8,128)S(1)}, u32[]{:S(2)}, u32[]{:S(2)}) collective-permute-start(f32[5,2048]{1,0:T(8,128)S(1)} %get-tuple-element.23), channel_id=1, source_target_pairs={{0,16},{16,32},{32,48},{48,64},{64,80},{80,96},{96,112},{112,128},... | collective-permute-start | bytes 122888 | tf_op jit(solution)/shard_map/ppermute | solution.py:25
  7.5 0.1 broadcast_and_fusion
  7.6 1.1 collective-permute-done
  8.9 5.1 %collective-permute-start.2 = (f32[42,5]{1,0:T(8,128)S(1)}, f32[42,5]{1,0:T(8,128)S(1)}, u32[]{:S(2)}, u32[]{:S(2)}) collective-permute-start(f32[42,5]{1,0:T(8,128)S(1)} %get-tuple-element.22), channel_id=1, source_target_pairs={{0,1},{1,2},{2,3},{3,4},{4,5},{5,6},{6,7},{7,8},{8,9},{9,10},{10,1... | collective-permute-start | bytes 2528 | tf_op jit(solution)/shard_map/ppermute | solution.py:25
  14.0 5.5 %collective-permute-start.3 = (f32[42,5]{1,0:T(8,128)S(1)}, f32[42,5]{1,0:T(8,128)S(1)}, u32[]{:S(2)}, u32[]{:S(2)}) collective-permute-start(f32[42,5]{1,0:T(8,128)S(1)} %get-tuple-element.21), channel_id=1, source_target_pairs={{1,0},{2,1},{3,2},{4,3},{5,4},{6,5},{7,6},{8,7},{9,8},{10,9},{11,1... | collective-permute-start | bytes 2528 | tf_op jit(solution)/shard_map/ppermute | solution.py:26
  19.5 0.1 broadcast_and_fusion.1
  19.6 0.7 collective-permute-done.3
  20.3 0.3 concatenate.79
  20.6 0.2 slice_subtract_fusion.14
  20.8 0.1 fusion.9
  21.0 0.1 fusion.5
  21.2 0.2 fusion.45
  21.5 0.2 fusion.46
  21.9 0.2 slice_subtract_fusion.12
  22.1 0.1 fusion.10
  22.2 0.1 fusion.6
  22.3 0.1 fusion
  22.5 0.2 fusion.36
  22.6 0.2 broadcast_multiply_fusion.2
  22.9 0.3 multiply_subtract_fusion.2
  23.2 0.2 slice_subtract_fusion.10
  23.4 0.1 fusion.11
  23.6 0.1 fusion.7
  23.7 0.2 fusion.1
  23.9 0.2 fusion.28
  24.1 0.3 broadcast_multiply_fusion.1
  24.5 0.4 multiply_subtract_fusion.1
  24.8 0.2 slice_subtract_fusion.8
  25.1 0.1 fusion.12
  25.2 0.1 fusion.8
  25.3 0.3 fusion.2
  25.6 0.2 fusion.20
  25.8 0.4 broadcast_multiply_fusion
  26.3 0.2 slice_subtract_fusion.6
  26.5 0.2 slice_subtract_fusion.4
  26.7 0.3 add_multiply_fusion
  27.0 0.2 slice_subtract_fusion.2
  27.3 0.2 slice_subtract_fusion
  27.5 2.0 %fusion.76 = (f32[]{:T(128)}, f32[]{:T(128)}, f32[]{:T(128)}, f32[]{:T(128)}, f32[32,2048]{1,0:T(8,128)}) fusion(f32[32,2048]{1,0:T(8,128)S(1)} %copy-done, f32[42,2058]{1,0:T(8,128)S(1)} %get-tuple-element.11, f32[42,2058]{1,0:T(8,128)S(1)} %get-tuple-element.12, f32[42,2058]{1,0:T(8,128)S(1)} %get-tuple-element.20, f32[42,2058]{1,0:T(8,128)S(1)} %get-tuple-element.18, ...), kind=kLoop, calls=%fused_computation.149 | loop fusion | flops 2359292 | bytes 2621456 | tf_op jit(solution)/shard_map/reduce_sum | solution.py:38
  29.5 1.6 %fusion.80 = (f32[]{:T(128)}, f32[]{:T(128)}, f32[]{:T(128)}, f32[]{:T(128)}) fusion(f32[42,2057]{1,0:T(8,128)S(1)} %slice_subtract_fusion.6, f32[41,2058]{1,0:T(8,128)S(1)} %slice_subtract_fusion.7, pred[42,2058]{1,0:T(8,128)(4,1)S(1)} %broadcast_and_fusion, pred[42,2058]{1,0:T(8,128)(4,1)S(1)} %broadcast_and_fusion.1, ...), kind=kLoop, calls=%fused_computation.154 | loop fusion | flops 1572860 | bytes 2863440 | tf_op jit(solution)/shard_map/reduce_sum | solution.py:38
  36.3 36.1 %psum.35 = f32[4]{0:T(128)S(1)} all-reduce(f32[4]{0:T(128)S(1)} %pad_maximum_fusion.2), channel_id=1, replica_groups=mesh['row_0'=8,'row_1'=4,'col_0'=2,'col_1'=4,'col_2'=2] {'row_0'}, use_global_device_ids=true, to_apply=%region_8.0 | all-reduce | flops 4 | bytes 32 | tf_op jit(solution)/shard_map/psum | solution.py:33
  72.4 6.0 %psum.36 = f32[4]{0:T(128)S(1)} all-reduce(f32[4]{0:T(128)S(1)} %psum.35), channel_id=1, replica_groups=mesh['row_0'=8,'row_1'=4,'col_0'=2,'col_1'=4,'col_2'=2] {'row_1'}, use_global_device_ids=true, to_apply=%region_9.0 | all-reduce | flops 4 | bytes 32 | tf_op jit(solution)/shard_map/psum | solution.py:33
  78.3 12.5 %psum.37 = f32[4]{0:T(128)S(1)} all-reduce(f32[4]{0:T(128)S(1)} %psum.36), channel_id=1, replica_groups=mesh['row_0'=8,'row_1'=4,'col_0'=2,'col_1'=4,'col_2'=2] {'col_0'}, use_global_device_ids=true, to_apply=%region_10.0 | all-reduce | flops 4 | bytes 32 | tf_op jit(solution)/shard_map/psum | solution.py:33
  90.8 24.8 %psum.38 = f32[4]{0:T(128)S(1)} all-reduce(f32[4]{0:T(128)S(1)} %psum.37), channel_id=1, replica_groups=mesh['row_0'=8,'row_1'=4,'col_0'=2,'col_1'=4,'col_2'=2] {'col_1'}, use_global_device_ids=true, to_apply=%region_11.0 | all-reduce | flops 4 | bytes 32 | tf_op jit(solution)/shard_map/psum | solution.py:33
  115.6 2.5 %psum.39 = f32[4]{0:T(128)S(1)} all-reduce(f32[4]{0:T(128)S(1)} %psum.38), channel_id=1, replica_groups=mesh['row_0'=8,'row_1'=4,'col_0'=2,'col_1'=4,'col_2'=2] {'col_2'}, use_global_device_ids=true, to_apply=%region_12.0 | all-reduce | flops 4 | bytes 32 | tf_op jit(solution)/shard_map/psum | solution.py:33
  118.1 0.5 broadcast_multiply_fusion.5
  (29 shorter events, 1.1 us)
Async XLA Ops:
  0.6 8.1 %copy-start = (f32[32,2048]{1,0:T(8,128)S(1)}, f32[32,2048]{1,0:T(8,128)}, u32[]{:S(2)}) copy-start(f32[32,2048]{1,0:T(8,128)} %param.1) | copy-start | bytes 786436
  1.6 6.0 %collective-permute-start.1 = (f32[5,2048]{1,0:T(8,128)S(1)}, f32[5,2048]{1,0:T(8,128)S(1)}, u32[]{:S(2)}, u32[]{:S(2)}) collective-permute-start(f32[5,2048]{1,0:T(8,128)S(1)} %get-tuple-element.24), channel_id=1, source_target_pairs={{16,0},{32,16},{48,32},{64,48},{80,64},{96,80},{112,96},{128,112},... | collective-permute-start | bytes 122888 | tf_op jit(solution)/shard_map/ppermute | solution.py:26
  2.9 5.9 %collective-permute-start = (f32[5,2048]{1,0:T(8,128)S(1)}, f32[5,2048]{1,0:T(8,128)S(1)}, u32[]{:S(2)}, u32[]{:S(2)}) collective-permute-start(f32[5,2048]{1,0:T(8,128)S(1)} %get-tuple-element.23), channel_id=1, source_target_pairs={{0,16},{16,32},{32,48},{48,64},{64,80},{80,96},{96,112},{112,128},... | collective-permute-start | bytes 122888 | tf_op jit(solution)/shard_map/ppermute | solution.py:25
  8.9 10.7 %collective-permute-start.2 = (f32[42,5]{1,0:T(8,128)S(1)}, f32[42,5]{1,0:T(8,128)S(1)}, u32[]{:S(2)}, u32[]{:S(2)}) collective-permute-start(f32[42,5]{1,0:T(8,128)S(1)} %get-tuple-element.22), channel_id=1, source_target_pairs={{0,1},{1,2},{2,3},{3,4},{4,5},{5,6},{6,7},{7,8},{8,9},{9,10},{10,1... | collective-permute-start | bytes 2528 | tf_op jit(solution)/shard_map/ppermute | solution.py:25
  14.0 6.3 %collective-permute-start.3 = (f32[42,5]{1,0:T(8,128)S(1)}, f32[42,5]{1,0:T(8,128)S(1)}, u32[]{:S(2)}, u32[]{:S(2)}) collective-permute-start(f32[42,5]{1,0:T(8,128)S(1)} %get-tuple-element.21), channel_id=1, source_target_pairs={{1,0},{2,1},{3,2},{4,3},{5,4},{6,5},{7,6},{8,7},{9,8},{10,9},{11,1... | collective-permute-start | bytes 2528 | tf_op jit(solution)/shard_map/ppermute | solution.py:26
where the time goes:
time: 119 us
  blocking collectives  81.8 us (69%)
  starting transfers between devices  16.4 us (14%)
  other arithmetic  11 us (9%)
  between operations  6.05 us (5%)
  waiting for transfers between devices  1.83 us (2%)
  local copies, waits for them, and re-layouts  1.49 us (1%)
    psum x5, blocking collectives, by_axis(): shard = lax.psum(shard, axis)  81.8 us
    ppermute x2, starting transfers between devices, with_halo(): before = lax.ppermute(last, axis, up)  9.7 us
    ppermute x2, starting transfers between devices, with_halo(): after = lax.ppermute(first, axis, down)  6.75 us
  transfers between devices with their start and end apart: 4, of which 2 were waited for; matrix products, arithmetic and copies ran while one was open for 0% of the time, Pallas kernels for 0%

commit v1 on v0

v1 whole, which is shorter than its diff:
```python
import jax
import jax.numpy as jnp
from jax import lax
from jax.experimental import pallas as pl
from jax.experimental.pallas import tpu as pltpu
from jax.sharding import PartitionSpec as P

ITERS = 4
Z_LO, X, Z_HI, Y = 8, 4, 2, 4
Z = Z_HI * Z_LO
N_ROW, N_COL = Z_LO * X, Z_HI * Y * 2
ROOTS = X * Y
TR, TC = 32, 2048
NT = TC // 128
FR = 40
BASE = 8
BUF = 56
TOP = 4
STRIP = NT
EDGE = 8

FIDELITY = 8.0
PSTEP = 0.35
DSTEP = 0.35
KA = 1.0 / (1.0 + PSTEP * FIDELITY)
KB = PSTEP / (1.0 + PSTEP * FIDELITY)
KC = PSTEP * FIDELITY / (1.0 + PSTEP * FIDELITY)
CELLS = float(N_ROW * TR * N_COL * TC)
TINY = 1e-37

SIDES = [(dr, dc) for dr in (-1, 0, 1) for dc in (-1, 0, 1) if (dr, dc) != (0, 0)]


def kernel(
    noisy, out, gap, own, top, bot, lef, rig, corners, nf, nc, xs, pr, pc, er, ec, gr, gc,
    msg, part, plane, result, own_sem, send_sem, recv_sem, part_send, part_recv, plane_send, plane_recv,
    result_send, result_recv,
):
    f32 = jnp.float32
    row, col = lax.axis_index("row"), lax.axis_index("col")
    zl, x = row // X, row % X
    zh, y, core = col // (2 * Y), (col // 2) % Y, col % 2
    z = zh * Z_LO + zl
    lane = lax.broadcasted_iota(jnp.int32, (FR, 128), 1)
    sub = lax.broadcasted_iota(jnp.int32, (FR, 128), 0)
    is_root = (z == 0) & (core == 1)
    early = col == 2 * Y - 1
    late = col == 2 * Y

    def ident(r, c):
        return r * N_COL + c

    def exists(dr, dc):
        cond = None
        for t in ([row >= 1] if dr < 0 else [row < N_ROW - 1] if dr > 0 else []) + (
            [col >= 1] if dc < 0 else [col < N_COL - 1] if dc > 0 else []
        ):
            cond = t if cond is None else cond & t
        return cond

    root_id = ident(x, y * 2 + 1)
    own_copy = pltpu.make_async_copy(noisy, own, own_sem)
    own_copy.start()

    barrier = pltpu.get_barrier_semaphore()

    def signal(target):
        pl.semaphore_signal(barrier, inc=1, device_id=target, device_id_type=pl.DeviceIdType.LOGICAL)

    heard = []
    for dr, dc in SIDES:
        greet = exists(dr, dc)
        if dc < 0:
            greet = greet & jnp.logical_not(late)
        pl.when(greet)(lambda dr=dr, dc=dc: signal(ident(row + dr, col + dc)))
        hear = exists(dr, dc)
        if dc > 0:
            hear = hear & jnp.logical_not(early)
        heard.append(hear)

    @pl.when(is_root)
    def _():
        for i in range(ROOTS):
            xx, yy = i // Y, i % Y

            @pl.when((x != xx) | (y != yy))
            def _():
                signal(ident(xx, yy * 2 + 1))

        signal(ident(row, col - 1))

        @pl.loop(1, Z)
        def _(zz):
            r, c = lax.rem(zz, Z_LO) * X + x, ((zz // Z_LO) * Y + y) * 2
            signal(ident(r, c))
            signal(ident(r, c + 1))


    for cond, buf in ((row == 0, top), (row == N_ROW - 1, bot), (col == 0, lef), (col == N_COL - 1, rig)):

        @pl.when(cond)
        def _():
            buf[...] = jnp.zeros_like(buf)

    for i, (dr, dc) in enumerate([(-1, -1), (-1, 1), (1, -1), (1, 1)]):

        @pl.when(jnp.logical_not(exists(dr, dc)))
        def _():
            corners[i] = jnp.zeros((8, 128), f32)

    for ref in (xs, pr):
        for t in range(NT + 1):
            ref[t, 0:BASE, :] = jnp.zeros((BASE, 128), f32)
            ref[t, BASE + FR : BUF, :] = jnp.zeros((BUF - BASE - FR, 128), f32)

    own_copy.wait()
    count = jnp.where(is_root, ROOTS - 1, 1)
    for hear in heard:
        count = count + jnp.where(hear, 1, 0)
    pl.semaphore_wait(barrier, count)

    place = {
        (-1, 0): top, (1, 0): bot, (0, -1): lef, (0, 1): rig, (-1, -1): corners.at[0], (-1, 1): corners.at[1],
        (1, -1): corners.at[2], (1, 1): corners.at[3],
    }

    def source(dr, dc):
        rs = slice(0, TR) if dr == 0 else slice(0, 8) if dr < 0 else slice(TR - 8, TR)
        cs = slice(0, TC) if dc == 0 else slice(0, 128) if dc < 0 else slice(TC - 128, TC)
        return own.at[rs, cs]

    def halo(dr, dc):
        i = SIDES.index((dr, dc))
        return pltpu.make_async_remote_copy(
            source(dr, dc), place[(-dr, -dc)], send_sem.at[i], recv_sem.at[SIDES.index((-dr, -dc))],
            device_id=ident(row + dr, col + dc), device_id_type=pl.DeviceIdType.LOGICAL,
        )

    def arrived(dr, dc):
        i = SIDES.index((dr, dc))
        return pltpu.make_async_remote_copy(
            source(-dr, -dc), place[(dr, dc)], send_sem.at[i], recv_sem.at[i],
            device_id=ident(row, col), device_id_type=pl.DeviceIdType.LOGICAL,
        )

    for dr, dc in [(1, 0), (-1, 0), (0, 1), (0, -1), (1, 1), (1, -1), (-1, 1), (-1, -1)]:
        cond = exists(dr, dc)
        if dc > 0:
            cond = cond & jnp.logical_not(early)
        pl.when(cond)(lambda dr=dr, dc=dc: halo(dr, dc).start())

    grow = row * TR - TOP + sub
    row_mask = jnp.where((grow >= 0) & (grow < N_ROW * TR - 1), DSTEP, 0.0).astype(f32)
    rows_in = (sub >= TOP) & (sub < TOP + TR)

    def frame(ref, t, shift=0):
        return ref[t, BASE + shift : BASE + shift + FR, :]

    def left_of(v):
        return pltpu.roll(v, 1, 1)

    def right_of(v):
        return pltpu.roll(v, 127, 1)

    def sums(cell):
        acc = cell[0:8]
        for i in range(1, FR // 8):
            acc = acc + cell[8 * i : 8 * i + 8]
        return acc

    def sweeps(tiles, col_mask, keep):
        acc_a, acc_b = [], []
        for k in range(ITERS):
            a_sum = b_sum = None
            prev_pc = None
            pend = None
            rolled_n = None
            for t in tiles + [None]:
                if t is not None:
                    n = frame(nf, t)
                    if k == 0:
                        ncol = right_of(n) if rolled_n is None else rolled_n
                        if t != tiles[-1]:
                            rolled_n = right_of(frame(nf, t + 1))
                            nright = jnp.where(lane == 127, rolled_n, ncol)
                        else:
                            nright = ncol
                        qr = (frame(nf, t, 1) - n) * row_mask
                        qc = (nright - n) * col_mask
                        gr[t] = qr
                        gc[t] = qc
                    else:
                        qr = frame(pr, t) + er[t]
                        qc = pc[t] + ec[t]
                    shrink = lax.rsqrt(jnp.maximum(qr * qr + qc * qc, 1.0))
                    p_r = qr * shrink
                    p_c = qc * shrink
                    pr[t, BASE : BASE + FR, :] = p_r
                    if k < ITERS - 1:
                        pc[t] = p_c
                    rolled = left_of(p_c)
                    pleft = rolled if prev_pc is None else jnp.where(lane == 0, prev_pc, rolled)
                    prev_pc = rolled
                    d = (p_r - frame(pr, t, -1)) + (p_c - pleft)
                    if k == 0:
                        new = n + KB * d
                        nc[t] = n * KC
                    else:
                        new = KA * frame(xs, t) + (KB * d + nc[t])
                    xs[t, BASE : BASE + FR, :] = new
                    rolled_x = right_of(new)
                if pend is not None:
                    s, sx, sd, sn, srolled = pend
                    xright = srolled if t is None else jnp.where(lane == 127, rolled_x, srolled)
                    g_r = (frame(xs, s, 1) - sx) * row_mask
                    g_c = (xright - sx) * col_mask
                    if k < ITERS - 1:
                        er[s] = g_r + (g_r - gr[s])
                        ec[s] = g_c + (g_c - gc[s])
                        gr[s] = g_r
                        gc[s] = g_c
                    m = g_r * g_r + g_c * g_c
                    size = m * lax.rsqrt(jnp.maximum(m, TINY))
                    diff = sx - sn
                    rest = (diff * diff) * (0.5 * FIDELITY) + sd * (sn + sd * (0.5 / FIDELITY))
                    mask = keep(s)
                    size = sums(jnp.where(mask, size, 0.0))
                    rest = sums(jnp.where(mask, rest, 0.0))
                    a_sum = size if a_sum is None else a_sum + size
                    b_sum = rest if b_sum is None else b_sum + rest
                if t is not None:
                    pend = (t, new, d, n, rolled_x)
            acc_a.append(a_sum)
            acc_b.append(b_sum)
        return acc_a, acc_b

    def wait_side(dr, dc, extra=None):
        cond = exists(dr, dc)
        if extra is not None:
            cond = cond & extra
        pl.when(cond)(lambda: arrived(dr, dc).wait_recv())

    wait_side(-1, 0)
    wait_side(1, 0)
    for t in range(NT):
        cs = slice(128 * t, 128 * t + 128)
        nf[t, BASE + TOP - 8 : BASE + TOP, :] = top[:, cs]
        nf[t, BASE + TOP : BASE + TOP + TR, :] = own[:, cs]
        nf[t, BASE + TOP + TR : BASE + TOP + TR + 8, :] = bot[:, cs]

    def keep_main(t):
        if t == 0:
            return rows_in & (lane >= EDGE)
        if t == NT - 1:
            return rows_in & (lane < 128 - EDGE)
        return rows_in

    acc_a, acc_b = sweeps(list(range(NT)), DSTEP, keep_main)

    for dr in (-1, 0, 1):
        wait_side(dr, -1, jnp.logical_not(late))
        wait_side(dr, 1)

    for dr in (-1, 0, 1):
        pl.when(exists(dr, 1) & early)(lambda dr=dr: halo(dr, 1).start())

    def pack(last, right, left, first):
        q = lax.broadcasted_iota(jnp.int32, last.shape, 1)
        v = jnp.where(q < 32, pltpu.roll(last, 32, 1), pltpu.roll(right, 32, 1))
        w = jnp.where(q < 96, pltpu.roll(left, 96, 1), pltpu.roll(first, 96, 1))
        return jnp.where(q < 64, v, w)

    def strip_frame(with_left):
        def part_of(ref, i=None):
            return ref[...] if i is None else ref[i]

        def left_part(ref, i, like):
            return part_of(ref, i) if with_left else jnp.zeros_like(like)

        lo, hi = slice(0, 128), slice(TC - 128, TC)
        t_right, m_right, b_right = corners[1], rig[...], corners[3]
        nf[STRIP, BASE + TOP - 8 : BASE + TOP, :] = pack(top[:, hi], t_right, left_part(corners, 0, t_right), top[:, lo])
        nf[STRIP, BASE + TOP : BASE + TOP + TR, :] = pack(own[:, hi], m_right, left_part(lef, None, m_right), own[:, lo])
        nf[STRIP, BASE + TOP + TR : BASE + TOP + TR + 8, :] = pack(bot[:, hi], b_right, left_part(corners, 2, b_right), bot[:, lo])

    pl.when(late)(lambda: strip_frame(False))
    pl.when(jnp.logical_not(late))(lambda: strip_frame(True))
    outside = ((col == 0) & (lane >= 64) & (lane < 96)) | ((col == N_COL - 1) & (lane >= 31) & (lane < 64))
    strip_mask = jnp.where(outside, 0.0, DSTEP).astype(f32)
    owned = ((lane >= 32 - EDGE) & (lane < 32)) | (early & (lane >= 32) & (lane < 32 + EDGE))
    owned = owned | (jnp.logical_not(late) & (lane >= 96) & (lane < 96 + EDGE))
    owned = owned & rows_in
    strip_a, strip_b = sweeps([STRIP], strip_mask, lambda t: owned)

    lane8 = lax.broadcasted_iota(jnp.int32, (8, 128), 1)
    sub8 = lax.broadcasted_iota(jnp.int32, (8, 128), 0)
    table = jnp.zeros((8, 128), f32)
    for k in range(ITERS):
        total = (acc_a[k] + strip_a[k]) * (1.0 / DSTEP) + (acc_b[k] + strip_b[k])
        table = jnp.where(sub8 == k, jnp.sum(total, axis=0, keepdims=True), table)
    line = jnp.sum(table, axis=1, keepdims=True)
    line = jnp.sum(jnp.where(lane8 == sub8, line, 0.0), axis=0, keepdims=True)
    msg[...] = line

    slot = z * 2 + core
    part_copy = pltpu.make_async_remote_copy(
        msg, part.at[slot], part_send, part_recv, device_id=root_id, device_id_type=pl.DeviceIdType.LOGICAL
    )
    pl.when(jnp.logical_not(is_root))(lambda: part_copy.start())

    lane32 = lax.broadcasted_iota(jnp.int32, (TR, 128), 1)
    for t in range(NT):
        v = xs[t, BASE + TOP : BASE + TOP + TR, :]
        if t in (0, NT - 1):
            s = xs[STRIP, BASE + TOP : BASE + TOP + TR, :]
            if t == 0:
                v = jnp.where(lane32 < EDGE, pltpu.roll(s, 32, 1), v)
            else:
                v = jnp.where(lane32 >= 128 - EDGE, pltpu.roll(s, 96, 1), v)
        out[:, 128 * t : 128 * t + 128] = v

    @pl.when(late)
    def _():
        for dr in (-1, 0, 1):
            wait_side(dr, -1)
        strip_frame(True)
        sweeps([STRIP], strip_mask, lambda t: owned)
        s = xs[STRIP, BASE + TOP : BASE + TOP + TR, :]
        out[:, 0:128] = jnp.where(lane32 < EDGE, pltpu.roll(s, 32, 1), out[:, 0:128])

    def rows_of(ref, n, sem):
        return pltpu.make_async_copy(ref.at[0:n], ref.at[0:n], sem)

    @pl.when(is_root)
    def _():
        rows_of(part, 2 * Z - 1, part_recv).wait()
        part[1] = msg[...]
        total = part[0]
        for i in range(1, 2 * Z):
            total = total + part[i]
        me = x * Y + y
        plane[me] = total
        for i in range(ROOTS):
            xx, yy = i // Y, i % Y

            @pl.when((x != xx) | (y != yy))
            def _():
                pltpu.make_async_remote_copy(
                    plane.at[me], plane.at[me], plane_send, plane_recv,
                    device_id=ident(xx, yy * 2 + 1), device_id_type=pl.DeviceIdType.LOGICAL,
                ).start()

        rows_of(plane, ROOTS - 1, plane_recv).wait()
        total = plane[0]
        for i in range(1, ROOTS):
            total = total + plane[i]
        result[...] = total * (1.0 / CELLS)

        def tell(target):
            pltpu.make_async_remote_copy(
                result, result, result_send, result_recv, device_id=target, device_id_type=pl.DeviceIdType.LOGICAL
            ).start()

        tell(ident(row, col - 1))

        @pl.loop(1, Z)
        def _(zz):
            r, c = lax.rem(zz, Z_LO) * X + x, ((zz // Z_LO) * Y + y) * 2
            tell(ident(r, c))
            tell(ident(r, c + 1))

        gap[...] = result[...]
        rows_of(plane, ROOTS - 1, plane_send).wait()
        rows_of(part, 2 * Z - 1, result_send).wait()

    @pl.when(jnp.logical_not(is_root))
    def _():
        pltpu.make_async_copy(result, result, result_recv).wait()
        gap[...] = result[...]
        part_copy.wait_send()

    for dr, dc in SIDES:
        pl.when(exists(dr, dc))(lambda dr=dr, dc=dc: halo(dr, dc).wait_send())


def on_device(noisy):
    f32 = jnp.float32
    vmem = pl.BlockSpec(memory_space=pltpu.VMEM)
    frame = lambda rows: pltpu.VMEM((NT + 1, rows, 128), f32)
    dma = pltpu.SemaphoreType.DMA
    denoised, gap = pl.pallas_call(
        kernel,
        out_shape=(jax.ShapeDtypeStruct((TR, TC), f32), jax.ShapeDtypeStruct((1, 128), f32)),
        in_specs=[pl.BlockSpec(memory_space=pltpu.HBM)],
        out_specs=(vmem, vmem),
        scratch_shapes=[
            pltpu.VMEM((TR, TC), f32),
            pltpu.VMEM((8, TC), f32),
            pltpu.VMEM((8, TC), f32),
            pltpu.VMEM((TR, 128), f32),
            pltpu.VMEM((TR, 128), f32),
            pltpu.VMEM((4, 8, 128), f32),
            frame(BUF), frame(FR), frame(BUF), frame(BUF), frame(FR), frame(FR), frame(FR), frame(FR), frame(FR),
            pltpu.VMEM((1, 128), f32),
            pltpu.VMEM((2 * Z, 1, 128), f32),
            pltpu.VMEM((ROOTS, 1, 128), f32),
            pltpu.VMEM((1, 128), f32),
            dma, dma((8,)), dma((8,)), dma, dma, dma, dma, dma, dma,
        ],
        compiler_params=pltpu.CompilerParams(
            collective_id=0, has_side_effects=True, vmem_limit_bytes=16 * 1024 * 1024
        ),
    )(noisy)
    return denoised, gap[0, :ITERS]


def solution(mesh):
    return jax.shard_map(
        on_device,
        mesh=mesh,
        in_specs=(P("row", "col"),),
        out_specs=(P("row", "col"), P()),
        check_vma=False,
    )
```

time: 119 us -> 39.9 us (0.34)
  blocking collectives: 81.8 us -> 0 us
  Pallas kernels: 0 us -> 36.9 us
  starting transfers between devices: 16.4 us -> 0 us
  other arithmetic: 11 us -> 0 us
  between operations: 6.05 us -> 0.65 us
  waiting for transfers between devices: 1.83 us -> 0 us
    psum x5 -> x0, blocking collectives: 81.8 us -> none  [by_axis(): shard = lax.psum(shard, axis)]
    pallas_call x0 -> x1, Pallas kernels: none -> 36.9 us  [on_device(): pl.pallas_call(kernel, out_shape=(jax.ShapeDtypeStruct((TR, TC), f32), ja...]
    ppermute x4 -> x0, starting transfers between devices: 16.4 us -> none  [the longest x2 9.7 us: with_halo(): before = lax.ppermute(last, axis, up)]
    reduce_sum x2 -> x0, other arithmetic: 3.66 us -> none  [the longest x1 2.03 us: gap_piece(): jnp.sum(0.5 * fidelity * (primal - noisy) ** 2 + noisy * diverged + diver...]
    sub x20 -> x0, other arithmetic: 2.56 us -> none  [the longest x8 1.39 us: masked_grads(): field[:, 1:] - field[:, :-1]]
    ppermute x4 -> x0, waiting for transfers between devices: 1.83 us -> none  [the longest x2 1.13 us: with_halo(): before = lax.ppermute(last, axis, up)]
    mul x9 -> x0, other arithmetic: 1.68 us -> none  [the longest x8 1.6 us: deep_run(): dual = trial * shrink]
    unnamed x2 -> x3, local copies, waits for them, and re-layouts: 0.01 us -> 1.65 us
  transfers between devices with their start and end apart: 4 -> 0, of which waited for: 2 -> 0; matrix products, arithmetic and copies ran while one was open for 0% -> 0% of each run, Pallas kernels for 0% -> 0%
where the time goes in v1:
time: 39.9 us; the launch traced here: 39.7 us
  Pallas kernels  36.9 us (92%)
  local copies, waits for them, and re-layouts  2.16 us (5%)
  between operations  0.65 us (2%)
    pallas_call x1, Pallas kernels, on_device(): pl.pallas_call(kernel, out_shape=(jax.ShapeDtypeStruct((TR, TC), f32), ja...  36.9 us
    unnamed x3, local copies, waits for them, and re-layouts  1.65 us

profile of v1, /device:TPU:1, one launch (start us, length us, event | category | flops | bytes accessed | tf_op | source)
XLA Modules:
  0.0 39.7 jit_solution(10168857268644713604)
XLA Ops:
  0.6 0.0 copy-start
  0.6 0.9 %copy-done = f32[32,2048]{1,0:T(8,128)S(1)} copy-done((f32[32,2048]{1,0:T(8,128)S(1)}, f32[32,2048]{1,0:T(8,128)}, u32[]{:S(2)}) %copy-start) | copy-done | bytes 262168
  1.6 36.9 %shard_map.30 = (f32[32,2048]{1,0:T(8,128)S(1)}, f32[1,128]{1,0:T(1,128)S(1)}) custom-call(f32[32,2048]{1,0:T(8,128)S(1)} %copy-done), custom_call_target="tpu_custom_call" | custom-call | tf_op jit(solution)/shard_map/pallas_call | solution.py:391
  38.5 0.5 %slice_bitcast_fusion = f32[4]{0:T(128)} fusion(f32[1,128]{1,0:T(1,128)S(1)} %get-tuple-element.5), kind=kLoop, calls=%fused_computation | loop fusion | bytes 32 | tf_op jit(solution)/shard_map/squeeze | solution.py:414
  39.0 0.7 %copy.4 = f32[32,2048]{1,0:T(8,128)} copy(f32[32,2048]{1,0:T(8,128)S(1)} %get-tuple-element.8) | data formatting | bytes 524288
Async XLA Ops:
  0.6 1.0 %copy-start = (f32[32,2048]{1,0:T(8,128)S(1)}, f32[32,2048]{1,0:T(8,128)}, u32[]{:S(2)}) copy-start(f32[32,2048]{1,0:T(8,128)} %noisy.1) | copy-start | bytes 786436

commit v2 on v1

--- a/solution.py
+++ b/solution.py
@@ -17,6 +17,7 @@
 BUF = 56
 TOP = 4
 STRIP = NT
+SEAM = NT + 1
 EDGE = 8
 
 FIDELITY = 8.0
@@ -32,9 +33,9 @@
 
 
 def kernel(
-    noisy, out, gap, own, top, bot, lef, rig, corners, nf, nc, xs, pr, pc, er, ec, gr, gc,
+    noisy, out, gap, own, top, bot, lef, rig, corners, seam_mid, seam_up, seam_down, seam_out, seam_in, nf, nc, xs, pr, pc, er, ec, gr, gc,
     msg, part, plane, result, own_sem, send_sem, recv_sem, part_send, part_recv, plane_send, plane_recv,
-    result_send, result_recv,
+    result_send, result_recv, seam_send, seam_recv, back_send, back_recv,
 ):
     f32 = jnp.float32
     row, col = lax.axis_index("row"), lax.axis_index("col")
@@ -44,14 +45,18 @@
     lane = lax.broadcasted_iota(jnp.int32, (FR, 128), 1)
     sub = lax.broadcasted_iota(jnp.int32, (FR, 128), 0)
     is_root = (z == 0) & (core == 1)
-    early = col == 2 * Y - 1
-    late = col == 2 * Y
+    before, after = col == 2 * Y - 1, col == 2 * Y
+    hub = z == 0
+    hub_row = col * X + x
 
     def ident(r, c):
         return r * N_COL + c
 
+    def hub_of(r):
+        return ident(r % X, r // X)
+
     def exists(dr, dc):
-        cond = None
+        cond = jnp.logical_not(before if dc > 0 else after) if dc else None
         for t in ([row >= 1] if dr < 0 else [row < N_ROW - 1] if dr > 0 else []) + (
             [col >= 1] if dc < 0 else [col < N_COL - 1] if dc > 0 else []
         ):
@@ -69,14 +74,16 @@
 
     heard = []
     for dr, dc in SIDES:
-        greet = exists(dr, dc)
-        if dc < 0:
-            greet = greet & jnp.logical_not(late)
-        pl.when(greet)(lambda dr=dr, dc=dc: signal(ident(row + dr, col + dc)))
-        hear = exists(dr, dc)
-        if dc > 0:
-            hear = hear & jnp.logical_not(early)
-        heard.append(hear)
+        pl.when(exists(dr, dc))(lambda dr=dr, dc=dc: signal(ident(row + dr, col + dc)))
+        heard.append(exists(dr, dc))
+
+    def row_in(r):
+        return (r >= 0) & (r < N_ROW)
+
+    for k in (-1, 0, 1):
+        for c in (2 * Y - 1, 2 * Y):
+            pl.when(hub & row_in(hub_row + k))(lambda k=k, c=c: signal(ident(hub_row + k, c)))
+        heard.append((before | after) & row_in(row + k))
 
     @pl.when(is_root)
     def _():
@@ -96,7 +103,11 @@
             signal(ident(r, c + 1))
 
 
-    for cond, buf in ((row == 0, top), (row == N_ROW - 1, bot), (col == 0, lef), (col == N_COL - 1, rig)):
+    gone = (
+        (row == 0, top), (row == N_ROW - 1, bot), ((col == 0) | after, lef), ((col == N_COL - 1) | before, rig),
+        (hub & (hub_row == 0), seam_up), (hub & (hub_row == N_ROW - 1), seam_down),
+    )
+    for cond, buf in gone:
 
         @pl.when(cond)
         def _():
@@ -109,7 +120,7 @@
             corners[i] = jnp.zeros((8, 128), f32)
 
     for ref in (xs, pr):
-        for t in range(NT + 1):
+        for t in range(NT + 2):
             ref[t, 0:BASE, :] = jnp.zeros((BASE, 128), f32)
             ref[t, BASE + FR : BUF, :] = jnp.zeros((BUF - BASE - FR, 128), f32)
 
@@ -144,13 +155,26 @@
         )
 
     for dr, dc in [(1, 0), (-1, 0), (0, 1), (0, -1), (1, 1), (1, -1), (-1, 1), (-1, -1)]:
-        cond = exists(dr, dc)
-        if dc > 0:
-            cond = cond & jnp.logical_not(early)
-        pl.when(cond)(lambda dr=dr, dc=dc: halo(dr, dc).start())
-
-    grow = row * TR - TOP + sub
-    row_mask = jnp.where((grow >= 0) & (grow < N_ROW * TR - 1), DSTEP, 0.0).astype(f32)
+        pl.when(exists(dr, dc))(lambda dr=dr, dc=dc: halo(dr, dc).start())
+
+    def to_hub(side, k):
+        ref = (seam_down, seam_mid, seam_up)[k + 1]
+        rs = (slice(0, 8), slice(0, TR), slice(TR - 8, TR))[k + 1]
+        cs = (slice(TC - 128, TC), slice(0, 128))[side]
+        i = side * 3 + k + 1
+        return pltpu.make_async_remote_copy(
+            own.at[rs, cs], ref.at[side], seam_send.at[k + 1], seam_recv.at[i],
+            device_id=hub_of(row + k), device_id_type=pl.DeviceIdType.LOGICAL,
+        )
+
+    for side, here in enumerate((before, after)):
+        for k in (0, -1, 1):
+            pl.when(here & row_in(row + k))(lambda side=side, k=k: to_hub(side, k).start())
+
+    def row_mask_of(r):
+        grow = r * TR - TOP + sub
+        return jnp.where((grow >= 0) & (grow < N_ROW * TR - 1), DSTEP, 0.0).astype(f32)
+
     rows_in = (sub >= TOP) & (sub < TOP + TR)
 
     def frame(ref, t, shift=0):
@@ -168,7 +192,7 @@
             acc = acc + cell[8 * i : 8 * i + 8]
         return acc
 
-    def sweeps(tiles, col_mask, keep):
+    def sweeps(tiles, row_mask, col_mask, keep):
         acc_a, acc_b = [], []
         for k in range(ITERS):
             a_sum = b_sum = None
@@ -234,11 +258,8 @@
             acc_b.append(b_sum)
         return acc_a, acc_b
 
-    def wait_side(dr, dc, extra=None):
-        cond = exists(dr, dc)
-        if extra is not None:
-            cond = cond & extra
-        pl.when(cond)(lambda: arrived(dr, dc).wait_recv())
+    def wait_side(dr, dc):
+        pl.when(exists(dr, dc))(lambda: arrived(dr, dc).wait_recv())
 
     wait_side(-1, 0)
     wait_side(1, 0)
@@ -255,58 +276,56 @@
             return rows_in & (lane < 128 - EDGE)
         return rows_in
 
-    acc_a, acc_b = sweeps(list(range(NT)), DSTEP, keep_main)
+    acc_a, acc_b = sweeps(list(range(NT)), row_mask_of(row), DSTEP, keep_main)
 
     for dr in (-1, 0, 1):
-        wait_side(dr, -1, jnp.logical_not(late))
+        wait_side(dr, -1)
         wait_side(dr, 1)
-
-    for dr in (-1, 0, 1):
-        pl.when(exists(dr, 1) & early)(lambda dr=dr: halo(dr, 1).start())
 
     def pack(last, right, left, first):
         q = lax.broadcasted_iota(jnp.int32, last.shape, 1)
         v = jnp.where(q < 32, pltpu.roll(last, 32, 1), pltpu.roll(right, 32, 1))
+        if left is None:
+            return v
         w = jnp.where(q < 96, pltpu.roll(left, 96, 1), pltpu.roll(first, 96, 1))
         return jnp.where(q < 64, v, w)
 
-    def strip_frame(with_left):
-        def part_of(ref, i=None):
-            return ref[...] if i is None else ref[i]
-
-        def left_part(ref, i, like):
-            return part_of(ref, i) if with_left else jnp.zeros_like(like)
-
-        lo, hi = slice(0, 128), slice(TC - 128, TC)
-        t_right, m_right, b_right = corners[1], rig[...], corners[3]
-        nf[STRIP, BASE + TOP - 8 : BASE + TOP, :] = pack(top[:, hi], t_right, left_part(corners, 0, t_right), top[:, lo])
-        nf[STRIP, BASE + TOP : BASE + TOP + TR, :] = pack(own[:, hi], m_right, left_part(lef, None, m_right), own[:, lo])
-        nf[STRIP, BASE + TOP + TR : BASE + TOP + TR + 8, :] = pack(bot[:, hi], b_right, left_part(corners, 2, b_right), bot[:, lo])
-
-    pl.when(late)(lambda: strip_frame(False))
-    pl.when(jnp.logical_not(late))(lambda: strip_frame(True))
+    def fill(t, parts):
+        nf[t, BASE + TOP - 8 : BASE + TOP, :] = parts[0]
+        nf[t, BASE + TOP : BASE + TOP + TR, :] = parts[1]
+        nf[t, BASE + TOP + TR : BASE + TOP + TR + 8, :] = parts[2]
+
+    lo, hi = slice(0, 128), slice(TC - 128, TC)
+    fill(STRIP, [
+        pack(top[:, hi], corners[1], corners[0], top[:, lo]),
+        pack(own[:, hi], rig[...], lef[...], own[:, lo]),
+        pack(bot[:, hi], corners[3], corners[2], bot[:, lo]),
+    ])
     outside = ((col == 0) & (lane >= 64) & (lane < 96)) | ((col == N_COL - 1) & (lane >= 31) & (lane < 64))
     strip_mask = jnp.where(outside, 0.0, DSTEP).astype(f32)
-    owned = ((lane >= 32 - EDGE) & (lane < 32)) | (early & (lane >= 32) & (lane < 32 + EDGE))
-    owned = owned | (jnp.logical_not(late) & (lane >= 96) & (lane < 96 + EDGE))
+    owned = jnp.logical_not(before) & (lane >= 32 - EDGE) & (lane < 32)
+    owned = owned | (jnp.logical_not(after) & (lane >= 96) & (lane < 96 + EDGE))
     owned = owned & rows_in
-    strip_a, strip_b = sweeps([STRIP], strip_mask, lambda t: owned)
+    strip_a, strip_b = sweeps([STRIP], row_mask_of(row), strip_mask, lambda t: owned)
 
     lane8 = lax.broadcasted_iota(jnp.int32, (8, 128), 1)
     sub8 = lax.broadcasted_iota(jnp.int32, (8, 128), 0)
-    table = jnp.zeros((8, 128), f32)
-    for k in range(ITERS):
-        total = (acc_a[k] + strip_a[k]) * (1.0 / DSTEP) + (acc_b[k] + strip_b[k])
-        table = jnp.where(sub8 == k, jnp.sum(total, axis=0, keepdims=True), table)
-    line = jnp.sum(table, axis=1, keepdims=True)
-    line = jnp.sum(jnp.where(lane8 == sub8, line, 0.0), axis=0, keepdims=True)
-    msg[...] = line
+
+    def line_of(a, b):
+        table = jnp.zeros((8, 128), f32)
+        for k in range(ITERS):
+            total = a[k] * (1.0 / DSTEP) + b[k]
+            table = jnp.where(sub8 == k, jnp.sum(total, axis=0, keepdims=True), table)
+        line = jnp.sum(table, axis=1, keepdims=True)
+        return jnp.sum(jnp.where(lane8 == sub8, line, 0.0), axis=0, keepdims=True)
+
+    msg[...] = line_of([p + q for p, q in zip(acc_a, strip_a)], [p + q for p, q in zip(acc_b, strip_b)])
 
     slot = z * 2 + core
     part_copy = pltpu.make_async_remote_copy(
         msg, part.at[slot], part_send, part_recv, device_id=root_id, device_id_type=pl.DeviceIdType.LOGICAL
     )
-    pl.when(jnp.logical_not(is_root))(lambda: part_copy.start())
+    pl.when(jnp.logical_not(hub))(lambda: part_copy.start())
 
     lane32 = lax.broadcasted_iota(jnp.int32, (TR, 128), 1)
     for t in range(NT):
@@ -319,14 +338,40 @@
                 v = jnp.where(lane32 >= 128 - EDGE, pltpu.roll(s, 96, 1), v)
         out[:, 128 * t : 128 * t + 128] = v
 
-    @pl.when(late)
+    def back(c):
+        return pltpu.make_async_remote_copy(
+            seam_out, seam_in, back_send.at[c - (2 * Y - 1)], back_recv,
+            device_id=ident(hub_row, c), device_id_type=pl.DeviceIdType.LOGICAL,
+        )
+
+    @pl.when(hub)
     def _():
-        for dr in (-1, 0, 1):
-            wait_side(dr, -1)
-        strip_frame(True)
-        sweeps([STRIP], strip_mask, lambda t: owned)
-        s = xs[STRIP, BASE + TOP : BASE + TOP + TR, :]
-        out[:, 0:128] = jnp.where(lane32 < EDGE, pltpu.roll(s, 32, 1), out[:, 0:128])
+        for side in (0, 1):
+            for k in (-1, 0, 1):
+                ref = (seam_up, seam_mid, seam_down)[k + 1]
+                i = side * 3 - k + 1
+
+                @pl.when(row_in(hub_row + k))
+                def _():
+                    pltpu.make_async_copy(ref.at[side], ref.at[side], seam_recv.at[i]).wait()
+
+        fill(SEAM, [pack(ref[0], ref[1], None, None) for ref in (seam_up, seam_mid, seam_down)])
+        inner = rows_in & (lane >= 32 - EDGE) & (lane < 32 + EDGE)
+        seam_a, seam_b = sweeps([SEAM], row_mask_of(hub_row), DSTEP, lambda t: inner)
+        seam_out[...] = xs[SEAM, BASE + TOP : BASE + TOP + TR, :]
+        msg[...] = msg[...] + line_of(seam_a, seam_b)
+        back(2 * Y - 1).start()
+        back(2 * Y).start()
+        pl.when(core != 1)(lambda: part_copy.start())
+
+    for here, lanes, cols in (
+        (before, lane32 >= 128 - EDGE, slice(TC - 128, TC)), (after, lane32 < EDGE, slice(0, 128))
+    ):
+
+        @pl.when(here)
+        def _():
+            pltpu.make_async_copy(seam_in, seam_in, back_recv).wait()
+            out[:, cols] = jnp.where(lanes, pltpu.roll(seam_in[...], 96, 1), out[:, cols])
 
     def rows_of(ref, n, sem):
         return pltpu.make_async_copy(ref.at[0:n], ref.at[0:n], sem)
@@ -381,12 +426,20 @@
 
     for dr, dc in SIDES:
         pl.when(exists(dr, dc))(lambda dr=dr, dc=dc: halo(dr, dc).wait_send())
+    for side, here in enumerate((before, after)):
+        for k in (-1, 0, 1):
+            pl.when(here & row_in(row + k))(lambda side=side, k=k: to_hub(side, k).wait_send())
+
+    @pl.when(hub)
+    def _():
+        back(2 * Y - 1).wait_send()
+        back(2 * Y).wait_send()
 
 
 def on_device(noisy):
     f32 = jnp.float32
     vmem = pl.BlockSpec(memory_space=pltpu.VMEM)
-    frame = lambda rows: pltpu.VMEM((NT + 1, rows, 128), f32)
+    frame = lambda rows: pltpu.VMEM((NT + 2, rows, 128), f32)
     dma = pltpu.SemaphoreType.DMA
     denoised, gap = pl.pallas_call(
         kernel,
@@ -400,17 +453,22 @@
             pltpu.VMEM((TR, 128), f32),
             pltpu.VMEM((TR, 128), f32),
             pltpu.VMEM((4, 8, 128), f32),
+            pltpu.VMEM((2, TR, 128), f32),
+            pltpu.VMEM((2, 8, 128), f32),
+            pltpu.VMEM((2, 8, 128), f32),
+            pltpu.VMEM((TR, 128), f32),
+            pltpu.VMEM((TR, 128), f32),
             frame(BUF), frame(FR), frame(BUF), frame(BUF), frame(FR), frame(FR), frame(FR), frame(FR), frame(FR),
             pltpu.VMEM((1, 128), f32),
             pltpu.VMEM((2 * Z, 1, 128), f32),
             pltpu.VMEM((ROOTS, 1, 128), f32),
             pltpu.VMEM((1, 128), f32),
-            dma, dma((8,)), dma((8,)), dma, dma, dma, dma, dma, dma,
+            dma, dma((8,)), dma((8,)), dma, dma, dma, dma, dma, dma, dma((3,)), dma((6,)), dma((2,)), dma,
         ],
         compiler_params=pltpu.CompilerParams(
             collective_id=0, has_side_effects=True, vmem_limit_bytes=16 * 1024 * 1024
         ),
-    )(noisy)
+    )(pltpu.with_memory_space_constraint(noisy, pltpu.HBM))
     return denoised, gap[0, :ITERS]
 
 

time: 39.9 us -> 37.8 us (0.947)
  Pallas kernels: 36.9 us -> 35.8 us
  local copies, waits for them, and re-layouts: 2.16 us -> 1.22 us
    pallas_call x1, Pallas kernels: 36.9 us -> 35.8 us  [on_device(): pl.pallas_call(kernel, out_shape=(jax.ShapeDtypeStruct((TR, TC), f32), ja...]
    unnamed x3 -> x1, local copies, waits for them, and re-layouts: 1.65 us -> 0.7 us
where the time goes in v2:
time: 37.8 us; the launch traced here: 37.7 us
  Pallas kernels  35.8 us (95%)
  local copies, waits for them, and re-layouts  1.22 us (3%)
  between operations  0.64 us (2%)
    pallas_call x1, Pallas kernels, on_device(): pl.pallas_call(kernel, out_shape=(jax.ShapeDtypeStruct((TR, TC), f32), ja...  35.8 us

profile of v2, /device:TPU:1, one launch (start us, length us, event | category | flops | bytes accessed | tf_op | source)
XLA Modules:
  0.0 37.7 jit_solution(14598615942139801575)
XLA Ops:
  0.6 35.8 %shard_map.30 = (f32[32,2048]{1,0:T(8,128)S(1)}, f32[1,128]{1,0:T(1,128)S(1)}) custom-call(f32[32,2048]{1,0:T(8,128)} %noisy.1), custom_call_target="tpu_custom_call" | custom-call | tf_op jit(solution)/shard_map/pallas_call | solution.py:444
  36.5 0.5 %slice_bitcast_fusion = f32[4]{0:T(128)} fusion(f32[1,128]{1,0:T(1,128)S(1)} %get-tuple-element.5), kind=kLoop, calls=%fused_computation | loop fusion | bytes 32 | tf_op jit(solution)/shard_map/squeeze | solution.py:472
  37.0 0.7 %copy.4 = f32[32,2048]{1,0:T(8,128)} copy(f32[32,2048]{1,0:T(8,128)S(1)} %get-tuple-element.8) | data formatting | bytes 524288

commit v3 on v2

--- a/solution.py
+++ b/solution.py
@@ -34,7 +34,7 @@
 
 def kernel(
     noisy, out, gap, own, top, bot, lef, rig, corners, seam_mid, seam_up, seam_down, seam_out, seam_in, nf, nc, xs, pr, pc, er, ec, gr, gc,
-    msg, part, plane, result, own_sem, send_sem, recv_sem, part_send, part_recv, plane_send, plane_recv,
+    msg, part, result, own_sem, send_sem, recv_sem, part_send, part_recv,
     result_send, result_recv, seam_send, seam_recv, back_send, back_recv,
 ):
     f32 = jnp.float32
@@ -63,7 +63,6 @@
             cond = t if cond is None else cond & t
         return cond
 
-    root_id = ident(x, y * 2 + 1)
     own_copy = pltpu.make_async_copy(noisy, own, own_sem)
     own_copy.start()
 
@@ -87,21 +86,17 @@
 
     @pl.when(is_root)
     def _():
-        for i in range(ROOTS):
-            xx, yy = i // Y, i % Y
-
-            @pl.when((x != xx) | (y != yy))
-            def _():
-                signal(ident(xx, yy * 2 + 1))
-
-        signal(ident(row, col - 1))
-
-        @pl.loop(1, Z)
-        def _(zz):
-            r, c = lax.rem(zz, Z_LO) * X + x, ((zz // Z_LO) * Y + y) * 2
-            signal(ident(r, c))
-            signal(ident(r, c + 1))
-
+        @pl.loop(0, Z - 1)
+        def _(i):
+            step = (i + 1) // 2
+            zz = jnp.where(i % 2 == 1, Z // 2 - step, Z // 2 + step)
+            for xx in range(X):
+                for yc in range(2 * Y):
+                    signal(ident((zz % Z_LO) * X + xx, (zz // Z_LO) * 2 * Y + yc))
+
+        for xx in range(X):
+            for yc in range(2 * Y):
+                pl.when((x != xx) | (y * 2 + 1 != yc))(lambda xx=xx, yc=yc: signal(ident(xx, yc)))
 
     gone = (
         (row == 0, top), (row == N_ROW - 1, bot), ((col == 0) | after, lef), ((col == N_COL - 1) | before, rig),
@@ -125,18 +120,20 @@
             ref[t, BASE + FR : BUF, :] = jnp.zeros((BUF - BASE - FR, 128), f32)
 
     own_copy.wait()
-    count = jnp.where(is_root, ROOTS - 1, 1)
+    count = jnp.where(is_root, ROOTS - 1, ROOTS)
     for hear in heard:
         count = count + jnp.where(hear, 1, 0)
     pl.semaphore_wait(barrier, count)
 
-    place = {
+    place0 = {
         (-1, 0): top, (1, 0): bot, (0, -1): lef, (0, 1): rig, (-1, -1): corners.at[0], (-1, 1): corners.at[1],
         (1, -1): corners.at[2], (1, 1): corners.at[3],
     }
 
+    place = {k: (v if k[0] == 0 else v.at[4:8] if k[0] < 0 else v.at[0:5]) for k, v in place0.items()}
+
     def source(dr, dc):
-        rs = slice(0, TR) if dr == 0 else slice(0, 8) if dr < 0 else slice(TR - 8, TR)
+        rs = slice(0, TR) if dr == 0 else slice(0, 5) if dr < 0 else slice(TR - 4, TR)
         cs = slice(0, TC) if dc == 0 else slice(0, 128) if dc < 0 else slice(TC - 128, TC)
         return own.at[rs, cs]
 
@@ -321,11 +318,20 @@
 
     msg[...] = line_of([p + q for p, q in zip(acc_a, strip_a)], [p + q for p, q in zip(acc_b, strip_b)])
 
-    slot = z * 2 + core
-    part_copy = pltpu.make_async_remote_copy(
-        msg, part.at[slot], part_send, part_recv, device_id=root_id, device_id_type=pl.DeviceIdType.LOGICAL
-    )
-    pl.when(jnp.logical_not(hub))(lambda: part_copy.start())
+    slot = ident(row, col)
+
+    def send_sums():
+        for i in range(ROOTS):
+            xx, yc = i // Y, i % Y * 2 + 1
+
+            @pl.when((row != xx) | (col != yc))
+            def _():
+                pltpu.make_async_remote_copy(
+                    msg, part.at[slot], part_send, part_recv,
+                    device_id=ident(xx, yc), device_id_type=pl.DeviceIdType.LOGICAL,
+                ).start()
+
+    pl.when(jnp.logical_not(hub))(send_sums)
 
     lane32 = lax.broadcasted_iota(jnp.int32, (TR, 128), 1)
     for t in range(NT):
@@ -362,7 +368,7 @@
         msg[...] = msg[...] + line_of(seam_a, seam_b)
         back(2 * Y - 1).start()
         back(2 * Y).start()
-        pl.when(core != 1)(lambda: part_copy.start())
+        send_sums()
 
     for here, lanes, cols in (
         (before, lane32 >= 128 - EDGE, slice(TC - 128, TC)), (after, lane32 < EDGE, slice(0, 128))
@@ -378,27 +384,9 @@
 
     @pl.when(is_root)
     def _():
-        rows_of(part, 2 * Z - 1, part_recv).wait()
-        part[1] = msg[...]
-        total = part[0]
-        for i in range(1, 2 * Z):
-            total = total + part[i]
-        me = x * Y + y
-        plane[me] = total
-        for i in range(ROOTS):
-            xx, yy = i // Y, i % Y
-
-            @pl.when((x != xx) | (y != yy))
-            def _():
-                pltpu.make_async_remote_copy(
-                    plane.at[me], plane.at[me], plane_send, plane_recv,
-                    device_id=ident(xx, yy * 2 + 1), device_id_type=pl.DeviceIdType.LOGICAL,
-                ).start()
-
-        rows_of(plane, ROOTS - 1, plane_recv).wait()
-        total = plane[0]
-        for i in range(1, ROOTS):
-            total = total + plane[i]
+        part[slot] = msg[...]
+        rows_of(part, N_ROW * N_COL - 1, part_recv).wait()
+        total = jnp.sum(part[...], axis=0)
         result[...] = total * (1.0 / CELLS)
 
         def tell(target):
@@ -415,14 +403,14 @@
             tell(ident(r, c + 1))
 
         gap[...] = result[...]
-        rows_of(plane, ROOTS - 1, plane_send).wait()
         rows_of(part, 2 * Z - 1, result_send).wait()
+        rows_of(part, ROOTS - 1, part_send).wait()
 
     @pl.when(jnp.logical_not(is_root))
     def _():
         pltpu.make_async_copy(result, result, result_recv).wait()
         gap[...] = result[...]
-        part_copy.wait_send()
+        rows_of(part, ROOTS, part_send).wait()
 
     for dr, dc in SIDES:
         pl.when(exists(dr, dc))(lambda dr=dr, dc=dc: halo(dr, dc).wait_send())
@@ -434,6 +422,11 @@
     def _():
         back(2 * Y - 1).wait_send()
         back(2 * Y).wait_send()
+
+
+def finish(denoised, line, out, gap):
+    out[...] = denoised[...]
+    gap[...] = line[0, :ITERS]
 
 
 def on_device(noisy):
@@ -460,16 +453,21 @@
             pltpu.VMEM((TR, 128), f32),
             frame(BUF), frame(FR), frame(BUF), frame(BUF), frame(FR), frame(FR), frame(FR), frame(FR), frame(FR),
             pltpu.VMEM((1, 128), f32),
-            pltpu.VMEM((2 * Z, 1, 128), f32),
-            pltpu.VMEM((ROOTS, 1, 128), f32),
+            pltpu.VMEM((N_ROW * N_COL, 1, 128), f32),
             pltpu.VMEM((1, 128), f32),
-            dma, dma((8,)), dma((8,)), dma, dma, dma, dma, dma, dma, dma((3,)), dma((6,)), dma((2,)), dma,
+            dma, dma((8,)), dma((8,)), dma, dma, dma, dma, dma((3,)), dma((6,)), dma((2,)), dma,
         ],
         compiler_params=pltpu.CompilerParams(
             collective_id=0, has_side_effects=True, vmem_limit_bytes=16 * 1024 * 1024
         ),
     )(pltpu.with_memory_space_constraint(noisy, pltpu.HBM))
-    return denoised, gap[0, :ITERS]
+    return pl.pallas_call(
+        finish,
+        out_shape=(jax.ShapeDtypeStruct((TR, TC), f32), jax.ShapeDtypeStruct((ITERS,), f32)),
+        in_specs=[vmem, vmem],
+        out_specs=(vmem, vmem),
+        compiler_params=pltpu.CompilerParams(vmem_limit_bytes=4 * 1024 * 1024),
+    )(denoised, gap)
 
 
 def solution(mesh):

time: 37.8 us -> 36.1 us (0.955)
  local copies, waits for them, and re-layouts: 1.22 us -> 0 us
  Pallas kernels: 35.8 us -> 35.3 us
    pallas_call x1, Pallas kernels: 35.8 us -> 34.5 us  [on_device(): pl.pallas_call(kernel, out_shape=(jax.ShapeDtypeStruct((TR, TC), f32), ja...]
    pallas_call x0 -> x1, Pallas kernels: none -> 0.72 us  [on_device(): pl.pallas_call(finish, out_shape=(jax.ShapeDtypeStruct((TR, TC), f32), ja...]
    unnamed x1 -> x0, local copies, waits for them, and re-layouts: 0.7 us -> none
    squeeze x1 -> x0, local copies, waits for them, and re-layouts: 0.51 us -> none  [on_device(): return (denoised, gap[0, :ITERS])]
where the time goes in v3:
time: 36.1 us; the launch traced here: 35.9 us
  Pallas kernels  35.3 us (98%)
  between operations  0.64 us (2%)
    pallas_call x1, Pallas kernels, on_device(): pl.pallas_call(kernel, out_shape=(jax.ShapeDtypeStruct((TR, TC), f32), ja...  34.5 us
    pallas_call x1, Pallas kernels, on_device(): pl.pallas_call(finish, out_shape=(jax.ShapeDtypeStruct((TR, TC), f32), ja...  0.72 us

profile of v3, /device:TPU:1, one launch (start us, length us, event | category | flops | bytes accessed | tf_op | source)
XLA Modules:
  0.0 35.9 jit_solution(4531225132737336100)
XLA Ops:
  0.6 34.5 %shard_map.30 = (f32[32,2048]{1,0:T(8,128)S(1)}, f32[1,128]{1,0:T(1,128)S(1)}) custom-call(f32[32,2048]{1,0:T(8,128)} %noisy.1), custom_call_target="tpu_custom_call" | custom-call | tf_op jit(solution)/shard_map/pallas_call | solution.py:437
  35.2 0.7 %shard_map.31 = (f32[32,2048]{1,0:T(8,128)}, f32[4]{0:T(128)}) custom-call(f32[32,2048]{1,0:T(8,128)S(1)} %get-tuple-element.4.denoised, f32[1,128]{1,0:T(1,128)S(1)} %get-tuple-element.5.line), custom_call_target="tpu_custom_call" | custom-call | tf_op jit(solution)/shard_map/pallas_call | solution.py:464

commit v4 on v3

--- a/solution.py
+++ b/solution.py
@@ -33,7 +33,7 @@
 
 
 def kernel(
-    noisy, out, gap, own, top, bot, lef, rig, corners, seam_mid, seam_up, seam_down, seam_out, seam_in, nf, nc, xs, pr, pc, er, ec, gr, gc,
+    noisy, out, gap, own, top, bot, lef, rig, corners, seam_mid, seam_up, seam_down, seam_out, seam_in, xs, pr, pc, er, ec, gr, gc,
     msg, part, result, own_sem, send_sem, recv_sem, part_send, part_recv,
     result_send, result_recv, seam_send, seam_recv, back_send, back_recv,
 ):
@@ -42,8 +42,13 @@
     zl, x = row // X, row % X
     zh, y, core = col // (2 * Y), (col // 2) % Y, col % 2
     z = zh * Z_LO + zl
-    lane = lax.broadcasted_iota(jnp.int32, (FR, 128), 1)
-    sub = lax.broadcasted_iota(jnp.int32, (FR, 128), 0)
+
+    def lane_of(wins):
+        return lax.broadcasted_iota(jnp.int32, (sum(n for _, n in wins), 128), 1)
+
+    def row_of(wins):
+        return jnp.concatenate([a + lax.broadcasted_iota(jnp.int32, (n, 128), 0) for a, n in wins], axis=0)
+
     is_root = (z == 0) & (core == 1)
     before, after = col == 2 * Y - 1, col == 2 * Y
     hub = z == 0
@@ -114,10 +119,9 @@
         def _():
             corners[i] = jnp.zeros((8, 128), f32)
 
-    for ref in (xs, pr):
+    for k in range(ITERS):
         for t in range(NT + 2):
-            ref[t, 0:BASE, :] = jnp.zeros((BASE, 128), f32)
-            ref[t, BASE + FR : BUF, :] = jnp.zeros((BUF - BASE - FR, 128), f32)
+            pr[k, t, 0:BASE, :] = jnp.zeros((BASE, 128), f32)
 
     own_copy.wait()
     count = jnp.where(is_root, ROOTS - 1, ROOTS)
@@ -168,14 +172,18 @@
         for k in (0, -1, 1):
             pl.when(here & row_in(row + k))(lambda side=side, k=k: to_hub(side, k).start())
 
-    def row_mask_of(r):
-        grow = r * TR - TOP + sub
+    def row_mask_of(r, wins):
+        grow = r * TR - TOP + row_of(wins)
         return jnp.where((grow >= 0) & (grow < N_ROW * TR - 1), DSTEP, 0.0).astype(f32)
 
-    rows_in = (sub >= TOP) & (sub < TOP + TR)
-
-    def frame(ref, t, shift=0):
-        return ref[t, BASE + shift : BASE + shift + FR, :]
+    def load(ref, k, t, wins, shift=0):
+        return jnp.concatenate([ref[k, t, BASE + a + shift : BASE + a + shift + n, :] for a, n in wins], axis=0)
+
+    def store(ref, k, t, wins, v):
+        at = 0
+        for a, n in wins:
+            ref[k, t, BASE + a : BASE + a + n, :] = v[at : at + n]
+            at += n
 
     def left_of(v):
         return pltpu.roll(v, 1, 1)
@@ -185,99 +193,108 @@
 
     def sums(cell):
         acc = cell[0:8]
-        for i in range(1, FR // 8):
+        for i in range(1, cell.shape[0] // 8):
             acc = acc + cell[8 * i : 8 * i + 8]
         return acc
 
-    def sweeps(tiles, row_mask, col_mask, keep):
-        acc_a, acc_b = [], []
-        for k in range(ITERS):
-            a_sum = b_sum = None
-            prev_pc = None
-            pend = None
-            rolled_n = None
-            for t in tiles + [None]:
-                if t is not None:
-                    n = frame(nf, t)
-                    if k == 0:
-                        ncol = right_of(n) if rolled_n is None else rolled_n
-                        if t != tiles[-1]:
-                            rolled_n = right_of(frame(nf, t + 1))
-                            nright = jnp.where(lane == 127, rolled_n, ncol)
-                        else:
-                            nright = ncol
-                        qr = (frame(nf, t, 1) - n) * row_mask
-                        qc = (nright - n) * col_mask
-                        gr[t] = qr
-                        gc[t] = qc
-                    else:
-                        qr = frame(pr, t) + er[t]
-                        qc = pc[t] + ec[t]
-                    shrink = lax.rsqrt(jnp.maximum(qr * qr + qc * qc, 1.0))
-                    p_r = qr * shrink
-                    p_c = qc * shrink
-                    pr[t, BASE : BASE + FR, :] = p_r
-                    if k < ITERS - 1:
-                        pc[t] = p_c
-                    rolled = left_of(p_c)
-                    pleft = rolled if prev_pc is None else jnp.where(lane == 0, prev_pc, rolled)
-                    prev_pc = rolled
-                    d = (p_r - frame(pr, t, -1)) + (p_c - pleft)
-                    if k == 0:
-                        new = n + KB * d
-                        nc[t] = n * KC
-                    else:
-                        new = KA * frame(xs, t) + (KB * d + nc[t])
-                    xs[t, BASE : BASE + FR, :] = new
-                    rolled_x = right_of(new)
-                if pend is not None:
-                    s, sx, sd, sn, srolled = pend
-                    xright = srolled if t is None else jnp.where(lane == 127, rolled_x, srolled)
-                    g_r = (frame(xs, s, 1) - sx) * row_mask
-                    g_c = (xright - sx) * col_mask
-                    if k < ITERS - 1:
-                        er[s] = g_r + (g_r - gr[s])
-                        ec[s] = g_c + (g_c - gc[s])
-                        gr[s] = g_r
-                        gc[s] = g_c
-                    m = g_r * g_r + g_c * g_c
-                    size = m * lax.rsqrt(jnp.maximum(m, TINY))
-                    diff = sx - sn
-                    rest = (diff * diff) * (0.5 * FIDELITY) + sd * (sn + sd * (0.5 / FIDELITY))
-                    mask = keep(s)
-                    size = sums(jnp.where(mask, size, 0.0))
-                    rest = sums(jnp.where(mask, rest, 0.0))
-                    a_sum = size if a_sum is None else a_sum + size
-                    b_sum = rest if b_sum is None else b_sum + rest
-                if t is not None:
-                    pend = (t, new, d, n, rolled_x)
-            acc_a.append(a_sum)
-            acc_b.append(b_sum)
-        return acc_a, acc_b
+    def sweep(k, tiles, wins, row_mask, col_mask, keep):
+        a_sum = b_sum = prev_pc = pend = rolled_n = None
+        lane = lane_of(wins)
+        for t in tiles + [None]:
+            if t is not None:
+                n = load(xs, 0, t, wins)
+                if k == 0:
+                    ncol = right_of(n) if rolled_n is None else rolled_n
+                    nright = ncol
+                    if t != tiles[-1]:
+                        rolled_n = right_of(load(xs, 0, t + 1, wins))
+                        nright = jnp.where(lane == 127, rolled_n, ncol)
+                    qr = (load(xs, 0, t, wins, 1) - n) * row_mask
+                    qc = (nright - n) * col_mask
+                    store(gr, 0, t, wins, qr)
+                    store(gc, 0, t, wins, qc)
+                else:
+                    qr = load(pr, k - 1, t, wins) + load(er, k - 1, t, wins)
+                    qc = load(pc, k - 1, t, wins) + load(ec, k - 1, t, wins)
+                shrink = lax.rsqrt(jnp.maximum(qr * qr + qc * qc, 1.0))
+                p_r = qr * shrink
+                p_c = qc * shrink
+                store(pr, k, t, wins, p_r)
+                if k < ITERS - 1:
+                    store(pc, k, t, wins, p_c)
+                rolled = left_of(p_c)
+                pleft = rolled if prev_pc is None else jnp.where(lane == 0, prev_pc, rolled)
+                prev_pc = rolled
+                d = (p_r - load(pr, k, t, wins, -1)) + (p_c - pleft)
+                if k == 0:
+                    new = n + KB * d
+                else:
+                    new = KA * load(xs, k, t, wins) + (KB * d + KC * n)
+                store(xs, k + 1, t, wins, new)
+                rolled_x = right_of(new)
+            if pend is not None:
+                s, sx, sd, sn, srolled = pend
+                xright = srolled if t is None else jnp.where(lane == 127, rolled_x, srolled)
+                g_r = (load(xs, k + 1, s, wins, 1) - sx) * row_mask
+                g_c = (xright - sx) * col_mask
+                if k < ITERS - 1:
+                    store(er, k, s, wins, g_r + (g_r - load(gr, k, s, wins)))
+                    store(ec, k, s, wins, g_c + (g_c - load(gc, k, s, wins)))
+                if k < ITERS - 2:
+                    store(gr, k + 1, s, wins, g_r)
+                    store(gc, k + 1, s, wins, g_c)
+                m = g_r * g_r + g_c * g_c
+                size = m * lax.rsqrt(jnp.maximum(m, TINY))
+                diff = sx - sn
+                rest = (diff * diff) * (0.5 * FIDELITY) + sd * (sn + sd * (0.5 / FIDELITY))
+                mask = keep(s, lane)
+                size = sums(jnp.where(mask, size, 0.0))
+                rest = sums(jnp.where(mask, rest, 0.0))
+                a_sum = size if a_sum is None else a_sum + size
+                b_sum = rest if b_sum is None else b_sum + rest
+            if t is not None:
+                pend = (t, new, d, n, rolled_x)
+        return a_sum, b_sum
 
     def wait_side(dr, dc):
         pl.when(exists(dr, dc))(lambda: arrived(dr, dc).wait_recv())
 
+    def columns(t, lane):
+        if t == 0:
+            return lane >= EDGE
+        if t == NT - 1:
+            return lane < 128 - EDGE
+        return None
+
+    def keep_rows(wins, first, last):
+        a = row_of(wins)
+        inside = (a >= TOP + first) & (a <= TOP + last)
+
+        def keep(t, lane):
+            here = columns(t, lane)
+            return inside if here is None else inside & here
+
+        return keep
+
+    MAIN = list(range(NT))
+    FULL = [(0, FR)]
+    INNER = [(TOP, TR)]
+    for t in MAIN:
+        xs[0, t, BASE + TOP : BASE + TOP + TR, :] = own[:, 128 * t : 128 * t + 128]
+    inner_mask = row_mask_of(row, INNER)
+    acc = []
+    for k in range(ITERS):
+        acc.append(sweep(k, MAIN, INNER, inner_mask, DSTEP, keep_rows(INNER, k + 1, TR - 3 - k)))
+
     wait_side(-1, 0)
     wait_side(1, 0)
-    for t in range(NT):
-        cs = slice(128 * t, 128 * t + 128)
-        nf[t, BASE + TOP - 8 : BASE + TOP, :] = top[:, cs]
-        nf[t, BASE + TOP : BASE + TOP + TR, :] = own[:, cs]
-        nf[t, BASE + TOP + TR : BASE + TOP + TR + 8, :] = bot[:, cs]
-
-    def keep_main(t):
-        if t == 0:
-            return rows_in & (lane >= EDGE)
-        if t == NT - 1:
-            return rows_in & (lane < 128 - EDGE)
-        return rows_in
-
-    acc_a, acc_b = sweeps(list(range(NT)), row_mask_of(row), DSTEP, keep_main)
-
     for dr in (-1, 0, 1):
         wait_side(dr, -1)
         wait_side(dr, 1)
+    for t in MAIN:
+        cs = slice(128 * t, 128 * t + 128)
+        xs[0, t, BASE + TOP - 8 : BASE + TOP, :] = top[:, cs]
+        xs[0, t, BASE + TOP + TR : BASE + TOP + TR + 8, :] = bot[:, cs]
 
     def pack(last, right, left, first):
         q = lax.broadcasted_iota(jnp.int32, last.shape, 1)
@@ -288,9 +305,9 @@
         return jnp.where(q < 64, v, w)
 
     def fill(t, parts):
-        nf[t, BASE + TOP - 8 : BASE + TOP, :] = parts[0]
-        nf[t, BASE + TOP : BASE + TOP + TR, :] = parts[1]
-        nf[t, BASE + TOP + TR : BASE + TOP + TR + 8, :] = parts[2]
+        xs[0, t, BASE + TOP - 8 : BASE + TOP, :] = parts[0]
+        xs[0, t, BASE + TOP : BASE + TOP + TR, :] = parts[1]
+        xs[0, t, BASE + TOP + TR : BASE + TOP + TR + 8, :] = parts[2]
 
     lo, hi = slice(0, 128), slice(TC - 128, TC)
     fill(STRIP, [
@@ -298,25 +315,39 @@
         pack(own[:, hi], rig[...], lef[...], own[:, lo]),
         pack(bot[:, hi], corners[3], corners[2], bot[:, lo]),
     ])
+    lane = lane_of(FULL)
     outside = ((col == 0) & (lane >= 64) & (lane < 96)) | ((col == N_COL - 1) & (lane >= 31) & (lane < 64))
     strip_mask = jnp.where(outside, 0.0, DSTEP).astype(f32)
+    rows_in = (row_of(FULL) >= TOP) & (row_of(FULL) < TOP + TR)
     owned = jnp.logical_not(before) & (lane >= 32 - EDGE) & (lane < 32)
     owned = owned | (jnp.logical_not(after) & (lane >= 96) & (lane < 96 + EDGE))
     owned = owned & rows_in
-    strip_a, strip_b = sweeps([STRIP], row_mask_of(row), strip_mask, lambda t: owned)
+    full_mask = row_mask_of(row, FULL)
+    for k in range(ITERS):
+        wins = [(k, 8), (32 - k, 8)]
+        rows = row_of(wins)
+        edge = ((rows >= TOP) & (rows <= TOP + k)) | ((rows >= TOP + TR - 2 - k) & (rows < TOP + TR))
+
+        def keep(t, lane, edge=edge):
+            here = columns(t, lane)
+            return edge if here is None else edge & here
+
+        outer = sweep(k, MAIN, wins, row_mask_of(row, wins), DSTEP, keep)
+        strip = sweep(k, [STRIP], FULL, full_mask, strip_mask, lambda t, lane: owned)
+        acc[k] = tuple(p + q + r for p, q, r in zip(acc[k], outer, strip))
 
     lane8 = lax.broadcasted_iota(jnp.int32, (8, 128), 1)
     sub8 = lax.broadcasted_iota(jnp.int32, (8, 128), 0)
 
-    def line_of(a, b):
+    def line_of(acc):
         table = jnp.zeros((8, 128), f32)
         for k in range(ITERS):
-            total = a[k] * (1.0 / DSTEP) + b[k]
+            total = acc[k][0] * (1.0 / DSTEP) + acc[k][1]
             table = jnp.where(sub8 == k, jnp.sum(total, axis=0, keepdims=True), table)
         line = jnp.sum(table, axis=1, keepdims=True)
         return jnp.sum(jnp.where(lane8 == sub8, line, 0.0), axis=0, keepdims=True)
 
-    msg[...] = line_of([p + q for p, q in zip(acc_a, strip_a)], [p + q for p, q in zip(acc_b, strip_b)])
+    msg[...] = line_of(acc)
 
     slot = ident(row, col)
 
@@ -335,9 +366,9 @@
 
     lane32 = lax.broadcasted_iota(jnp.int32, (TR, 128), 1)
     for t in range(NT):
-        v = xs[t, BASE + TOP : BASE + TOP + TR, :]
+        v = xs[ITERS, t, BASE + TOP : BASE + TOP + TR, :]
         if t in (0, NT - 1):
-            s = xs[STRIP, BASE + TOP : BASE + TOP + TR, :]
+            s = xs[ITERS, STRIP, BASE + TOP : BASE + TOP + TR, :]
             if t == 0:
                 v = jnp.where(lane32 < EDGE, pltpu.roll(s, 32, 1), v)
             else:
@@ -363,9 +394,10 @@
 
         fill(SEAM, [pack(ref[0], ref[1], None, None) for ref in (seam_up, seam_mid, seam_down)])
         inner = rows_in & (lane >= 32 - EDGE) & (lane < 32 + EDGE)
-        seam_a, seam_b = sweeps([SEAM], row_mask_of(hub_row), DSTEP, lambda t: inner)
-        seam_out[...] = xs[SEAM, BASE + TOP : BASE + TOP + TR, :]
-        msg[...] = msg[...] + line_of(seam_a, seam_b)
+        seam_mask = row_mask_of(hub_row, FULL)
+        seam = [sweep(k, [SEAM], FULL, seam_mask, DSTEP, lambda t, lane: inner) for k in range(ITERS)]
+        seam_out[...] = xs[ITERS, SEAM, BASE + TOP : BASE + TOP + TR, :]
+        msg[...] = msg[...] + line_of(seam)
         back(2 * Y - 1).start()
         back(2 * Y).start()
         send_sums()
@@ -386,7 +418,11 @@
     def _():
         part[slot] = msg[...]
         rows_of(part, N_ROW * N_COL - 1, part_recv).wait()
-        total = jnp.sum(part[...], axis=0)
+        step = N_ROW * N_COL // 16
+        total = [jnp.sum(part[step * i : step * i + step], axis=0) for i in range(16)]
+        while len(total) > 1:
+            total = [p + q for p, q in zip(total[::2], total[1::2])]
+        total = total[0]
         result[...] = total * (1.0 / CELLS)
 
         def tell(target):
@@ -432,7 +468,7 @@
 def on_device(noisy):
     f32 = jnp.float32
     vmem = pl.BlockSpec(memory_space=pltpu.VMEM)
-    frame = lambda rows: pltpu.VMEM((NT + 2, rows, 128), f32)
+    frame = lambda n: pltpu.VMEM((n, NT + 2, BUF, 128), f32)
     dma = pltpu.SemaphoreType.DMA
     denoised, gap = pl.pallas_call(
         kernel,
@@ -451,14 +487,14 @@
             pltpu.VMEM((2, 8, 128), f32),
             pltpu.VMEM((TR, 128), f32),
             pltpu.VMEM((TR, 128), f32),
-            frame(BUF), frame(FR), frame(BUF), frame(BUF), frame(FR), frame(FR), frame(FR), frame(FR), frame(FR),
+            frame(ITERS + 1), frame(ITERS), frame(ITERS), frame(ITERS), frame(ITERS), frame(ITERS), frame(ITERS),
             pltpu.VMEM((1, 128), f32),
             pltpu.VMEM((N_ROW * N_COL, 1, 128), f32),
             pltpu.VMEM((1, 128), f32),
             dma, dma((8,)), dma((8,)), dma, dma, dma, dma, dma((3,)), dma((6,)), dma((2,)), dma,
         ],
         compiler_params=pltpu.CompilerParams(
-            collective_id=0, has_side_effects=True, vmem_limit_bytes=16 * 1024 * 1024
+            collective_id=0, has_side_effects=True, vmem_limit_bytes=24 * 1024 * 1024
         ),
     )(pltpu.with_memory_space_constraint(noisy, pltpu.HBM))
     return pl.pallas_call(

time: 36.1 us -> 32.7 us (0.906)
  Pallas kernels: 35.3 us -> 31.9 us
    pallas_call x1, Pallas kernels: 34.5 us -> 31.2 us  [on_device(): pl.pallas_call(kernel, out_shape=(jax.ShapeDtypeStruct((TR, TC), f32), ja...]
where the time goes in v4:
time: 32.7 us; the launch traced here: 32.5 us
  Pallas kernels  31.9 us (98%)
  between operations  0.64 us (2%)
    pallas_call x1, Pallas kernels, on_device(): pl.pallas_call(kernel, out_shape=(jax.ShapeDtypeStruct((TR, TC), f32), ja...  31.2 us
    pallas_call x1, Pallas kernels, on_device(): pl.pallas_call(finish, out_shape=(jax.ShapeDtypeStruct((TR, TC), f32), ja...  0.72 us

profile of v4, /device:TPU:1, one launch (start us, length us, event | category | flops | bytes accessed | tf_op | source)
XLA Modules:
  0.0 32.5 jit_solution(11161242702942429214)
XLA Ops:
  0.6 31.2 %shard_map.30 = (f32[32,2048]{1,0:T(8,128)S(1)}, f32[1,128]{1,0:T(1,128)S(1)}) custom-call(f32[32,2048]{1,0:T(8,128)} %noisy.1), custom_call_target="tpu_custom_call" | custom-call | tf_op jit(solution)/shard_map/pallas_call | solution.py:473
  31.8 0.7 %shard_map.31 = (f32[32,2048]{1,0:T(8,128)}, f32[4]{0:T(128)}) custom-call(f32[32,2048]{1,0:T(8,128)S(1)} %get-tuple-element.4.denoised, f32[1,128]{1,0:T(1,128)S(1)} %get-tuple-element.5.line), custom_call_target="tpu_custom_call" | custom-call | tf_op jit(solution)/shard_map/pallas_call | solution.py:500

commit v5 on v4

--- a/solution.py
+++ b/solution.py
@@ -9,7 +9,8 @@
 Z_LO, X, Z_HI, Y = 8, 4, 2, 4
 Z = Z_HI * Z_LO
 N_ROW, N_COL = Z_LO * X, Z_HI * Y * 2
-ROOTS = X * Y
+ROOTS = [(0, 1), (0, 0), (X, 1), (X, 0)] + [(i // Y, i % Y * 2 + 1) for i in range(1, X * Y)]
+N_ROOTS = len(ROOTS)
 TR, TC = 32, 2048
 NT = TC // 128
 FR = 40
@@ -49,7 +50,8 @@
     def row_of(wins):
         return jnp.concatenate([a + lax.broadcasted_iota(jnp.int32, (n, 128), 0) for a, n in wins], axis=0)
 
-    is_root = (z == 0) & (core == 1)
+    origin = (x == 0) & (y == 0)
+    is_root = ((z == 0) & ((core == 1) | origin)) | ((z == 1) & origin)
     before, after = col == 2 * Y - 1, col == 2 * Y
     hub = z == 0
     hub_row = col * X + x
@@ -94,14 +96,14 @@
         @pl.loop(0, Z - 1)
         def _(i):
             step = (i + 1) // 2
-            zz = jnp.where(i % 2 == 1, Z // 2 - step, Z // 2 + step)
+            zz = (z + jnp.where(i % 2 == 1, Z // 2 - step, Z // 2 + step)) % Z
             for xx in range(X):
                 for yc in range(2 * Y):
                     signal(ident((zz % Z_LO) * X + xx, (zz // Z_LO) * 2 * Y + yc))
 
         for xx in range(X):
             for yc in range(2 * Y):
-                pl.when((x != xx) | (y * 2 + 1 != yc))(lambda xx=xx, yc=yc: signal(ident(xx, yc)))
+                pl.when((x != xx) | (y * 2 + core != yc))(lambda xx=xx, yc=yc: signal(ident(zl * X + xx, zh * 2 * Y + yc)))
 
     gone = (
         (row == 0, top), (row == N_ROW - 1, bot), ((col == 0) | after, lef), ((col == N_COL - 1) | before, rig),
@@ -124,7 +126,7 @@
             pr[k, t, 0:BASE, :] = jnp.zeros((BASE, 128), f32)
 
     own_copy.wait()
-    count = jnp.where(is_root, ROOTS - 1, ROOTS)
+    count = jnp.where(is_root, N_ROOTS - 1, N_ROOTS)
     for hear in heard:
         count = count + jnp.where(hear, 1, 0)
     pl.semaphore_wait(barrier, count)
@@ -337,23 +339,20 @@
         acc[k] = tuple(p + q + r for p, q, r in zip(acc[k], outer, strip))
 
     lane8 = lax.broadcasted_iota(jnp.int32, (8, 128), 1)
-    sub8 = lax.broadcasted_iota(jnp.int32, (8, 128), 0)
 
     def line_of(acc):
         table = jnp.zeros((8, 128), f32)
         for k in range(ITERS):
             total = acc[k][0] * (1.0 / DSTEP) + acc[k][1]
-            table = jnp.where(sub8 == k, jnp.sum(total, axis=0, keepdims=True), table)
-        line = jnp.sum(table, axis=1, keepdims=True)
-        return jnp.sum(jnp.where(lane8 == sub8, line, 0.0), axis=0, keepdims=True)
+            table = jnp.where(lane8 == k, jnp.sum(total, axis=1, keepdims=True), table)
+        return jnp.sum(table, axis=0, keepdims=True)
 
     msg[...] = line_of(acc)
 
     slot = ident(row, col)
 
     def send_sums():
-        for i in range(ROOTS):
-            xx, yc = i // Y, i % Y * 2 + 1
+        for xx, yc in ROOTS:
 
             @pl.when((row != xx) | (col != yc))
             def _():
@@ -430,23 +429,32 @@
                 result, result, result_send, result_recv, device_id=target, device_id_type=pl.DeviceIdType.LOGICAL
             ).start()
 
-        tell(ident(row, col - 1))
-
-        @pl.loop(1, Z)
-        def _(zz):
-            r, c = lax.rem(zz, Z_LO) * X + x, ((zz // Z_LO) * Y + y) * 2
-            tell(ident(r, c))
-            tell(ident(r, c + 1))
-
         gap[...] = result[...]
-        rows_of(part, 2 * Z - 1, result_send).wait()
-        rows_of(part, ROOTS - 1, part_send).wait()
+
+        def tell_planes(start, stop):
+            @pl.loop(start, stop)
+            def _(zz):
+                r, c = lax.rem(zz, Z_LO) * X + x, ((zz // Z_LO) * Y + y) * 2
+                tell(ident(r, c))
+                tell(ident(r, c + 1))
+
+            rows_of(part, 2 * (stop - start), result_send).wait()
+
+        pl.when(hub & (core == 0))(lambda: tell_planes(2, Z))
+
+        @pl.when(hub & (core == 1) & jnp.logical_not(origin))
+        def _():
+            tell(ident(row, col - 1))
+            tell_planes(1, Z)
+            rows_of(part, 1, result_send).wait()
+
+        rows_of(part, N_ROOTS - 1, part_send).wait()
 
     @pl.when(jnp.logical_not(is_root))
     def _():
         pltpu.make_async_copy(result, result, result_recv).wait()
         gap[...] = result[...]
-        rows_of(part, ROOTS, part_send).wait()
+        rows_of(part, N_ROOTS, part_send).wait()
 
     for dr, dc in SIDES:
         pl.when(exists(dr, dc))(lambda dr=dr, dc=dc: halo(dr, dc).wait_send())

time: 32.7 us -> 32 us (0.979); the launches traced: 32.5 us -> 31.5 us
  Pallas kernels: 31.9 us -> 30.8 us
    pallas_call x1, Pallas kernels: 31.2 us -> 30.1 us  [on_device(): pl.pallas_call(kernel, out_shape=(jax.ShapeDtypeStruct((TR, TC), f32), ja...]
where the time goes in v5:
time: 32 us; the launch traced here: 31.5 us
  Pallas kernels  30.8 us (96%)
  between operations  0.64 us (2%)
    pallas_call x1, Pallas kernels, on_device(): pl.pallas_call(kernel, out_shape=(jax.ShapeDtypeStruct((TR, TC), f32), ja...  30.1 us
    pallas_call x1, Pallas kernels, on_device(): pl.pallas_call(finish, out_shape=(jax.ShapeDtypeStruct((TR, TC), f32), ja...  0.72 us

profile of v5, /device:TPU:1, one launch (start us, length us, event | category | flops | bytes accessed | tf_op | source)
XLA Modules:
  0.0 31.5 jit_solution(3168983058458651899)
XLA Ops:
  0.6 30.1 %shard_map.30 = (f32[32,2048]{1,0:T(8,128)S(1)}, f32[1,128]{1,0:T(1,128)S(1)}) custom-call(f32[32,2048]{1,0:T(8,128)} %noisy.1), custom_call_target="tpu_custom_call" | custom-call | tf_op jit(solution)/shard_map/pallas_call | solution.py:481
  30.8 0.7 %shard_map.31 = (f32[32,2048]{1,0:T(8,128)}, f32[4]{0:T(128)}) custom-call(f32[32,2048]{1,0:T(8,128)S(1)} %get-tuple-element.4.denoised, f32[1,128]{1,0:T(1,128)S(1)} %get-tuple-element.5.line), custom_call_target="tpu_custom_call" | custom-call | tf_op jit(solution)/shard_map/pallas_call | solution.py:508

commit v6 on v5

--- a/solution.py
+++ b/solution.py
@@ -9,7 +9,9 @@
 Z_LO, X, Z_HI, Y = 8, 4, 2, 4
 Z = Z_HI * Z_LO
 N_ROW, N_COL = Z_LO * X, Z_HI * Y * 2
-ROOTS = [(0, 1), (0, 0), (X, 1), (X, 0)] + [(i // Y, i % Y * 2 + 1) for i in range(1, X * Y)]
+ALONE = 2
+ROOTS = [(0, 1), (0, 0)] + [(X * i, c) for i in range(1, ALONE + 1) for c in (1, 0)]
+ROOTS += [(i // Y, i % Y * 2 + 1) for i in range(1, X * Y)]
 N_ROOTS = len(ROOTS)
 TR, TC = 32, 2048
 NT = TC // 128
@@ -29,12 +31,14 @@
 KC = PSTEP * FIDELITY / (1.0 + PSTEP * FIDELITY)
 CELLS = float(N_ROW * TR * N_COL * TC)
 TINY = 1e-37
+INNER_SKEW = 20
+SKEW = 4
 
 SIDES = [(dr, dc) for dr in (-1, 0, 1) for dc in (-1, 0, 1) if (dr, dc) != (0, 0)]
 
 
 def kernel(
-    noisy, out, gap, own, top, bot, lef, rig, corners, seam_mid, seam_up, seam_down, seam_out, seam_in, xs, pr, pc, er, ec, gr, gc,
+    noisy, out, gap, own, top, bot, lef, rig, corners, seam_mid, seam_up, seam_down, seam_out, seam_in, xs, nc, pr, pc, er, ec, gr, gc,
     msg, part, result, own_sem, send_sem, recv_sem, part_send, part_recv,
     result_send, result_recv, seam_send, seam_recv, back_send, back_recv,
 ):
@@ -51,7 +55,7 @@
         return jnp.concatenate([a + lax.broadcasted_iota(jnp.int32, (n, 128), 0) for a, n in wins], axis=0)
 
     origin = (x == 0) & (y == 0)
-    is_root = ((z == 0) & ((core == 1) | origin)) | ((z == 1) & origin)
+    is_root = ((z == 0) & ((core == 1) | origin)) | ((z >= 1) & (z <= ALONE) & origin)
     before, after = col == 2 * Y - 1, col == 2 * Y
     hub = z == 0
     hub_row = col * X + x
@@ -70,8 +74,12 @@
             cond = t if cond is None else cond & t
         return cond
 
-    own_copy = pltpu.make_async_copy(noisy, own, own_sem)
-    own_copy.start()
+    own_copies = [
+        pltpu.make_async_copy(noisy.at[8 * i : 8 * i + 8], own.at[8 * i : 8 * i + 8], own_sem.at[i])
+        for i in range(TR // 8)
+    ]
+    for i in (0, 3, 1, 2):
+        own_copies[i].start()
 
     barrier = pltpu.get_barrier_semaphore()
 
@@ -125,7 +133,8 @@
         for t in range(NT + 2):
             pr[k, t, 0:BASE, :] = jnp.zeros((BASE, 128), f32)
 
-    own_copy.wait()
+    own_copies[0].wait()
+    own_copies[3].wait()
     count = jnp.where(is_root, N_ROOTS - 1, N_ROOTS)
     for hear in heard:
         count = count + jnp.where(hear, 1, 0)
@@ -157,7 +166,10 @@
             device_id=ident(row, col), device_id_type=pl.DeviceIdType.LOGICAL,
         )
 
-    for dr, dc in [(1, 0), (-1, 0), (0, 1), (0, -1), (1, 1), (1, -1), (-1, 1), (-1, -1)]:
+    for dr, dc in [(1, 1), (1, -1), (-1, 1), (-1, -1), (1, 0), (-1, 0), (0, 1), (0, -1)]:
+        if (dr, dc) == (0, 1):
+            own_copies[1].wait()
+            own_copies[2].wait()
         pl.when(exists(dr, dc))(lambda dr=dr, dc=dc: halo(dr, dc).start())
 
     def to_hub(side, k):
@@ -176,7 +188,7 @@
 
     def row_mask_of(r, wins):
         grow = r * TR - TOP + row_of(wins)
-        return jnp.where((grow >= 0) & (grow < N_ROW * TR - 1), DSTEP, 0.0).astype(f32)
+        return jnp.where((grow >= 0) & (grow < N_ROW * TR - 1), 1.0, 0.0).astype(f32)
 
     def load(ref, k, t, wins, shift=0):
         return jnp.concatenate([ref[k, t, BASE + a + shift : BASE + a + shift + n, :] for a, n in wins], axis=0)
@@ -200,7 +212,10 @@
         return acc
 
     def sweep(k, tiles, wins, row_mask, col_mask, keep):
-        a_sum = b_sum = prev_pc = pend = rolled_n = None
+        def masked(v, mask):
+            return v if mask is None else v * mask
+
+        total = prev_pc = pend = rolled_n = None
         lane = lane_of(wins)
         for t in tiles + [None]:
             if t is not None:
@@ -211,8 +226,8 @@
                     if t != tiles[-1]:
                         rolled_n = right_of(load(xs, 0, t + 1, wins))
                         nright = jnp.where(lane == 127, rolled_n, ncol)
-                    qr = (load(xs, 0, t, wins, 1) - n) * row_mask
-                    qc = (nright - n) * col_mask
+                    qr = masked(load(xs, 0, t, wins, 1) - n, row_mask)
+                    qc = masked(nright - n, col_mask)
                     store(gr, 0, t, wins, qr)
                     store(gc, 0, t, wins, qc)
                 else:
@@ -229,16 +244,17 @@
                 prev_pc = rolled
                 d = (p_r - load(pr, k, t, wins, -1)) + (p_c - pleft)
                 if k == 0:
-                    new = n + KB * d
+                    new = n + (KB * DSTEP) * d
+                    store(nc, 0, t, wins, n * KC)
                 else:
-                    new = KA * load(xs, k, t, wins) + (KB * d + KC * n)
+                    new = KA * load(xs, k, t, wins) + ((KB * DSTEP) * d + load(nc, 0, t, wins))
                 store(xs, k + 1, t, wins, new)
                 rolled_x = right_of(new)
             if pend is not None:
                 s, sx, sd, sn, srolled = pend
                 xright = srolled if t is None else jnp.where(lane == 127, rolled_x, srolled)
-                g_r = (load(xs, k + 1, s, wins, 1) - sx) * row_mask
-                g_c = (xright - sx) * col_mask
+                g_r = masked(load(xs, k + 1, s, wins, 1) - sx, row_mask)
+                g_c = masked(xright - sx, col_mask)
                 if k < ITERS - 1:
                     store(er, k, s, wins, g_r + (g_r - load(gr, k, s, wins)))
                     store(ec, k, s, wins, g_c + (g_c - load(gc, k, s, wins)))
@@ -248,15 +264,28 @@
                 m = g_r * g_r + g_c * g_c
                 size = m * lax.rsqrt(jnp.maximum(m, TINY))
                 diff = sx - sn
-                rest = (diff * diff) * (0.5 * FIDELITY) + sd * (sn + sd * (0.5 / FIDELITY))
-                mask = keep(s, lane)
-                size = sums(jnp.where(mask, size, 0.0))
-                rest = sums(jnp.where(mask, rest, 0.0))
-                a_sum = size if a_sum is None else a_sum + size
-                b_sum = rest if b_sum is None else b_sum + rest
+                cell = (diff * diff) * (0.5 * FIDELITY / DSTEP) + sd * (sn + sd * (0.5 * DSTEP / FIDELITY))
+                cell = sums(jnp.where(keep(s, lane), cell + size, 0.0))
+                total = cell if total is None else total + cell
             if t is not None:
                 pend = (t, new, d, n, rolled_x)
-        return a_sum, b_sum
+            yield
+        return total
+
+    def interleave(work):
+        work = [list(w) for w in work]
+        results = [None] * len(work)
+        step = 0
+        while any(g is not None for _, g in work):
+            for i, (start, g) in enumerate(work):
+                if g is not None and step >= start:
+                    try:
+                        next(g)
+                    except StopIteration as end:
+                        results[i] = end.value
+                        work[i][1] = None
+            step += 1
+        return results
 
     def wait_side(dr, dc):
         pl.when(exists(dr, dc))(lambda: arrived(dr, dc).wait_recv())
@@ -282,11 +311,11 @@
     FULL = [(0, FR)]
     INNER = [(TOP, TR)]
     for t in MAIN:
-        xs[0, t, BASE + TOP : BASE + TOP + TR, :] = own[:, 128 * t : 128 * t + 128]
-    inner_mask = row_mask_of(row, INNER)
-    acc = []
-    for k in range(ITERS):
-        acc.append(sweep(k, MAIN, INNER, inner_mask, DSTEP, keep_rows(INNER, k + 1, TR - 3 - k)))
+        xs[0, t, BASE + TOP : BASE + TOP + TR, :] = own[:, 128 * t : 128 * t + 128] * DSTEP
+    acc = interleave(
+        (k * INNER_SKEW, sweep(k, MAIN, INNER, None, None, keep_rows(INNER, k + 1, TR - 3 - k)))
+        for k in range(ITERS)
+    )
 
     wait_side(-1, 0)
     wait_side(1, 0)
@@ -295,8 +324,8 @@
         wait_side(dr, 1)
     for t in MAIN:
         cs = slice(128 * t, 128 * t + 128)
-        xs[0, t, BASE + TOP - 8 : BASE + TOP, :] = top[:, cs]
-        xs[0, t, BASE + TOP + TR : BASE + TOP + TR + 8, :] = bot[:, cs]
+        xs[0, t, BASE + TOP - 8 : BASE + TOP, :] = top[:, cs] * DSTEP
+        xs[0, t, BASE + TOP + TR : BASE + TOP + TR + 8, :] = bot[:, cs] * DSTEP
 
     def pack(last, right, left, first):
         q = lax.broadcasted_iota(jnp.int32, last.shape, 1)
@@ -307,9 +336,9 @@
         return jnp.where(q < 64, v, w)
 
     def fill(t, parts):
-        xs[0, t, BASE + TOP - 8 : BASE + TOP, :] = parts[0]
-        xs[0, t, BASE + TOP : BASE + TOP + TR, :] = parts[1]
-        xs[0, t, BASE + TOP + TR : BASE + TOP + TR + 8, :] = parts[2]
+        xs[0, t, BASE + TOP - 8 : BASE + TOP, :] = parts[0] * DSTEP
+        xs[0, t, BASE + TOP : BASE + TOP + TR, :] = parts[1] * DSTEP
+        xs[0, t, BASE + TOP + TR : BASE + TOP + TR + 8, :] = parts[2] * DSTEP
 
     lo, hi = slice(0, 128), slice(TC - 128, TC)
     fill(STRIP, [
@@ -319,12 +348,13 @@
     ])
     lane = lane_of(FULL)
     outside = ((col == 0) & (lane >= 64) & (lane < 96)) | ((col == N_COL - 1) & (lane >= 31) & (lane < 64))
-    strip_mask = jnp.where(outside, 0.0, DSTEP).astype(f32)
+    strip_mask = jnp.where(outside, 0.0, 1.0).astype(f32)
     rows_in = (row_of(FULL) >= TOP) & (row_of(FULL) < TOP + TR)
     owned = jnp.logical_not(before) & (lane >= 32 - EDGE) & (lane < 32)
     owned = owned | (jnp.logical_not(after) & (lane >= 96) & (lane < 96 + EDGE))
     owned = owned & rows_in
     full_mask = row_mask_of(row, FULL)
+    work = []
     for k in range(ITERS):
         wins = [(k, 8), (32 - k, 8)]
         rows = row_of(wins)
@@ -334,17 +364,17 @@
             here = columns(t, lane)
             return edge if here is None else edge & here
 
-        outer = sweep(k, MAIN, wins, row_mask_of(row, wins), DSTEP, keep)
-        strip = sweep(k, [STRIP], FULL, full_mask, strip_mask, lambda t, lane: owned)
-        acc[k] = tuple(p + q + r for p, q, r in zip(acc[k], outer, strip))
+        work.append((k * SKEW, sweep(k, MAIN, wins, row_mask_of(row, wins), None, keep)))
+        work.append((k * SKEW, sweep(k, [STRIP], FULL, full_mask, strip_mask, lambda t, lane: owned)))
+    done = interleave(work)
+    acc = [acc[k] + done[2 * k] + done[2 * k + 1] for k in range(ITERS)]
 
     lane8 = lax.broadcasted_iota(jnp.int32, (8, 128), 1)
 
     def line_of(acc):
         table = jnp.zeros((8, 128), f32)
         for k in range(ITERS):
-            total = acc[k][0] * (1.0 / DSTEP) + acc[k][1]
-            table = jnp.where(lane8 == k, jnp.sum(total, axis=1, keepdims=True), table)
+            table = jnp.where(lane8 == k, jnp.sum(acc[k], axis=1, keepdims=True), table)
         return jnp.sum(table, axis=0, keepdims=True)
 
     msg[...] = line_of(acc)
@@ -372,7 +402,7 @@
                 v = jnp.where(lane32 < EDGE, pltpu.roll(s, 32, 1), v)
             else:
                 v = jnp.where(lane32 >= 128 - EDGE, pltpu.roll(s, 96, 1), v)
-        out[:, 128 * t : 128 * t + 128] = v
+        out[:, 128 * t : 128 * t + 128] = v * (1.0 / DSTEP)
 
     def back(c):
         return pltpu.make_async_remote_copy(
@@ -394,8 +424,8 @@
         fill(SEAM, [pack(ref[0], ref[1], None, None) for ref in (seam_up, seam_mid, seam_down)])
         inner = rows_in & (lane >= 32 - EDGE) & (lane < 32 + EDGE)
         seam_mask = row_mask_of(hub_row, FULL)
-        seam = [sweep(k, [SEAM], FULL, seam_mask, DSTEP, lambda t, lane: inner) for k in range(ITERS)]
-        seam_out[...] = xs[ITERS, SEAM, BASE + TOP : BASE + TOP + TR, :]
+        seam = interleave((3 * k, sweep(k, [SEAM], FULL, seam_mask, None, lambda t, lane: inner)) for k in range(ITERS))
+        seam_out[...] = xs[ITERS, SEAM, BASE + TOP : BASE + TOP + TR, :] * (1.0 / DSTEP)
         msg[...] = msg[...] + line_of(seam)
         back(2 * Y - 1).start()
         back(2 * Y).start()
@@ -422,7 +452,7 @@
         while len(total) > 1:
             total = [p + q for p, q in zip(total[::2], total[1::2])]
         total = total[0]
-        result[...] = total * (1.0 / CELLS)
+        result[...] = total * (1.0 / (CELLS * DSTEP))
 
         def tell(target):
             pltpu.make_async_remote_copy(
@@ -440,7 +470,7 @@
 
             rows_of(part, 2 * (stop - start), result_send).wait()
 
-        pl.when(hub & (core == 0))(lambda: tell_planes(2, Z))
+        pl.when(hub & (core == 0))(lambda: tell_planes(ALONE + 1, Z))
 
         @pl.when(hub & (core == 1) & jnp.logical_not(origin))
         def _():
@@ -495,11 +525,11 @@
             pltpu.VMEM((2, 8, 128), f32),
             pltpu.VMEM((TR, 128), f32),
             pltpu.VMEM((TR, 128), f32),
-            frame(ITERS + 1), frame(ITERS), frame(ITERS), frame(ITERS), frame(ITERS), frame(ITERS), frame(ITERS),
+            frame(ITERS + 1), frame(1), frame(ITERS), frame(ITERS), frame(ITERS), frame(ITERS), frame(ITERS), frame(ITERS),
             pltpu.VMEM((1, 128), f32),
             pltpu.VMEM((N_ROW * N_COL, 1, 128), f32),
             pltpu.VMEM((1, 128), f32),
-            dma, dma((8,)), dma((8,)), dma, dma, dma, dma, dma((3,)), dma((6,)), dma((2,)), dma,
+            dma((4,)), dma((8,)), dma((8,)), dma, dma, dma, dma, dma((3,)), dma((6,)), dma((2,)), dma,
         ],
         compiler_params=pltpu.CompilerParams(
             collective_id=0, has_side_effects=True, vmem_limit_bytes=24 * 1024 * 1024

time: 32 us -> 31.5 us (0.984); the launches traced: 31.5 us -> 31.3 us
  no operation moved by 1% of the time
where the time goes in v6:
time: 31.5 us; the launch traced here: 31.3 us
  Pallas kernels  30.7 us (97%)
  between operations  0.64 us (2%)
    pallas_call x1, Pallas kernels, on_device(): pl.pallas_call(kernel, out_shape=(jax.ShapeDtypeStruct((TR, TC), f32), ja...  30 us
    pallas_call x1, Pallas kernels, on_device(): pl.pallas_call(finish, out_shape=(jax.ShapeDtypeStruct((TR, TC), f32), ja...  0.72 us

profile of v6, /device:TPU:1, one launch (start us, length us, event | category | flops | bytes accessed | tf_op | source)
XLA Modules:
  0.0 31.3 jit_solution(133743286274002816)
XLA Ops:
  0.6 30.0 %shard_map.30 = (f32[32,2048]{1,0:T(8,128)S(1)}, f32[1,128]{1,0:T(1,128)S(1)}) custom-call(f32[32,2048]{1,0:T(8,128)} %noisy.1), custom_call_target="tpu_custom_call" | custom-call | tf_op jit(solution)/shard_map/pallas_call | solution.py:511
  30.6 0.7 %shard_map.31 = (f32[32,2048]{1,0:T(8,128)}, f32[4]{0:T(128)}) custom-call(f32[32,2048]{1,0:T(8,128)S(1)} %get-tuple-element.4.denoised, f32[1,128]{1,0:T(1,128)S(1)} %get-tuple-element.5.line), custom_call_target="tpu_custom_call" | custom-call | tf_op jit(solution)/shard_map/pallas_call | solution.py:538

commit v7 on v6

--- a/solution.py
+++ b/solution.py
@@ -387,7 +387,7 @@
             @pl.when((row != xx) | (col != yc))
             def _():
                 pltpu.make_async_remote_copy(
-                    msg, part.at[slot], part_send, part_recv,
+                    msg, part.at[pl.ds(slot, 1)], part_send, part_recv,
                     device_id=ident(xx, yc), device_id_type=pl.DeviceIdType.LOGICAL,
                 ).start()
 
@@ -443,15 +443,28 @@
     def rows_of(ref, n, sem):
         return pltpu.make_async_copy(ref.at[0:n], ref.at[0:n], sem)
 
+    for dr, dc in SIDES:
+        pl.when(exists(dr, dc))(lambda dr=dr, dc=dc: halo(dr, dc).wait_send())
+    for side, here in enumerate((before, after)):
+        for k in (-1, 0, 1):
+            pl.when(here & row_in(row + k))(lambda side=side, k=k: to_hub(side, k).wait_send())
+
+    @pl.when(hub)
+    def _():
+        back(2 * Y - 1).wait_send()
+        back(2 * Y).wait_send()
+
+    pl.when(is_root)(lambda: rows_of(part, N_ROOTS - 1, part_send).wait())
+    pl.when(jnp.logical_not(is_root))(lambda: rows_of(part, N_ROOTS, part_send).wait())
+
     @pl.when(is_root)
     def _():
-        part[slot] = msg[...]
+        part[pl.ds(slot, 1), :] = msg[...]
         rows_of(part, N_ROW * N_COL - 1, part_recv).wait()
-        step = N_ROW * N_COL // 16
-        total = [jnp.sum(part[step * i : step * i + step], axis=0) for i in range(16)]
+        total = [part[8 * i : 8 * i + 8] for i in range(N_ROW * N_COL // 8)]
         while len(total) > 1:
             total = [p + q for p, q in zip(total[::2], total[1::2])]
-        total = total[0]
+        total = jnp.sum(total[0], axis=0, keepdims=True)
         result[...] = total * (1.0 / (CELLS * DSTEP))
 
         def tell(target):
@@ -478,24 +491,11 @@
             tell_planes(1, Z)
             rows_of(part, 1, result_send).wait()
 
-        rows_of(part, N_ROOTS - 1, part_send).wait()
 
     @pl.when(jnp.logical_not(is_root))
     def _():
         pltpu.make_async_copy(result, result, result_recv).wait()
         gap[...] = result[...]
-        rows_of(part, N_ROOTS, part_send).wait()
-
-    for dr, dc in SIDES:
-        pl.when(exists(dr, dc))(lambda dr=dr, dc=dc: halo(dr, dc).wait_send())
-    for side, here in enumerate((before, after)):
-        for k in (-1, 0, 1):
-            pl.when(here & row_in(row + k))(lambda side=side, k=k: to_hub(side, k).wait_send())
-
-    @pl.when(hub)
-    def _():
-        back(2 * Y - 1).wait_send()
-        back(2 * Y).wait_send()
 
 
 def finish(denoised, line, out, gap):
@@ -527,7 +527,7 @@
             pltpu.VMEM((TR, 128), f32),
             frame(ITERS + 1), frame(1), frame(ITERS), frame(ITERS), frame(ITERS), frame(ITERS), frame(ITERS), frame(ITERS),
             pltpu.VMEM((1, 128), f32),
-            pltpu.VMEM((N_ROW * N_COL, 1, 128), f32),
+            pltpu.VMEM((N_ROW * N_COL, 128), f32),
             pltpu.VMEM((1, 128), f32),
             dma((4,)), dma((8,)), dma((8,)), dma, dma, dma, dma, dma((3,)), dma((6,)), dma((2,)), dma,
         ],

time: 31.5 us -> 31.3 us (level)
  no operation moved by 1% of the time
where the time goes in v7:
time: 31.3 us; the launch traced here: 31.1 us
  Pallas kernels  30.5 us (97%)
  between operations  0.64 us (2%)
    pallas_call x1, Pallas kernels, on_device(): pl.pallas_call(kernel, out_shape=(jax.ShapeDtypeStruct((TR, TC), f32), ja...  29.8 us
    pallas_call x1, Pallas kernels, on_device(): pl.pallas_call(finish, out_shape=(jax.ShapeDtypeStruct((TR, TC), f32), ja...  0.72 us

profile of v7, /device:TPU:1, one launch (start us, length us, event | category | flops | bytes accessed | tf_op | source)
XLA Modules:
  0.0 31.1 jit_solution(2501435361286286840)
XLA Ops:
  0.6 29.8 %shard_map.30 = (f32[32,2048]{1,0:T(8,128)S(1)}, f32[1,128]{1,0:T(1,128)S(1)}) custom-call(f32[32,2048]{1,0:T(8,128)} %noisy.1), custom_call_target="tpu_custom_call" | custom-call | tf_op jit(solution)/shard_map/pallas_call | solution.py:511
  30.4 0.7 %shard_map.31 = (f32[32,2048]{1,0:T(8,128)}, f32[4]{0:T(128)}) custom-call(f32[32,2048]{1,0:T(8,128)S(1)} %get-tuple-element.4.denoised, f32[1,128]{1,0:T(1,128)S(1)} %get-tuple-element.5.line), custom_call_target="tpu_custom_call" | custom-call | tf_op jit(solution)/shard_map/pallas_call | solution.py:538

commit v8 on v7

--- a/solution.py
+++ b/solution.py
@@ -9,7 +9,7 @@
 Z_LO, X, Z_HI, Y = 8, 4, 2, 4
 Z = Z_HI * Z_LO
 N_ROW, N_COL = Z_LO * X, Z_HI * Y * 2
-ALONE = 2
+ALONE = 3
 ROOTS = [(0, 1), (0, 0)] + [(X * i, c) for i in range(1, ALONE + 1) for c in (1, 0)]
 ROOTS += [(i // Y, i % Y * 2 + 1) for i in range(1, X * Y)]
 N_ROOTS = len(ROOTS)

time: 31.3 us -> 31.3 us (level)
  no operation moved by 1% of the time
where the time goes in v8:
time: 31.3 us; the launch traced here: 31.1 us
  Pallas kernels  30.5 us (97%)
  between operations  0.64 us (2%)
    pallas_call x1, Pallas kernels, on_device(): pl.pallas_call(kernel, out_shape=(jax.ShapeDtypeStruct((TR, TC), f32), ja...  29.8 us
    pallas_call x1, Pallas kernels, on_device(): pl.pallas_call(finish, out_shape=(jax.ShapeDtypeStruct((TR, TC), f32), ja...  0.72 us

profile of v8, /device:TPU:1, one launch (start us, length us, event | category | flops | bytes accessed | tf_op | source)
XLA Modules:
  0.0 31.1 jit_solution(9063149291476760417)
XLA Ops:
  0.6 29.8 %shard_map.30 = (f32[32,2048]{1,0:T(8,128)S(1)}, f32[1,128]{1,0:T(1,128)S(1)}) custom-call(f32[32,2048]{1,0:T(8,128)} %noisy.1), custom_call_target="tpu_custom_call" | custom-call | tf_op jit(solution)/shard_map/pallas_call | solution.py:511
  30.4 0.7 %shard_map.31 = (f32[32,2048]{1,0:T(8,128)}, f32[4]{0:T(128)}) custom-call(f32[32,2048]{1,0:T(8,128)S(1)} %get-tuple-element.4.denoised, f32[1,128]{1,0:T(1,128)S(1)} %get-tuple-element.5.line), custom_call_target="tpu_custom_call" | custom-call | tf_op jit(solution)/shard_map/pallas_call | solution.py:538
